TPU v7x, 32 devices: a whole 2x2x4 slice. The times are simulated.
32 devices in a mesh: by: 4 (over z), bx: 8 (over y, x, core).
Axes of the slice: x: 2, y: 2, z: 4, core: 2. Of those that a mesh axis runs over, the one named last changes fastest.
Arguments:
- wave_fn: float32 [1024, 2, 2, 1024], P('bx', None, None, 'by')
- left_env: float32 [1024, 5, 1024], P('bx')
- mpo_ten: float32 [5, 2, 2, 5], replicated
- right_env: float32 [1024, 5, 1024], P('by')
Outputs:
- output: float32 [1024, 2, 2, 1024], P('bx', None, None, 'by')
All inputs are finite; a program needn't handle non-finite values.
Results may differ from a plain program's by a relative error of at most 0.001.
Values sent between devices are 32-bit elements.
A program may use at most 1 GiB of HBM per device.

v0:
```python
import jax
import jax.numpy as jnp
from jax import lax
from jax.sharding import PartitionSpec as P


def solution(mesh):
    prec_mode = lax.Precision.HIGHEST

    def local_apply(wave_blk, left_rows, mpo_ten, right_rows):
        row_share, mpo_dim, bond_dim = left_rows.shape
        phys_dim = wave_blk.shape[1]
        col_share = wave_blk.shape[3]
        wave_cols = lax.all_gather(wave_blk, 'bx', axis=0, tiled=True)
        stage_one = jnp.dot(left_rows.reshape(row_share * mpo_dim, bond_dim), wave_cols.reshape(bond_dim, phys_dim * phys_dim * col_share), precision=prec_mode, preferred_element_type=jnp.float32)
        stage_one = stage_one.reshape(row_share, mpo_dim, phys_dim, phys_dim, col_share)
        stage_two = jnp.einsum('aupqf,uspv->asvqf', stage_one, mpo_ten, precision=prec_mode, preferred_element_type=jnp.float32)
        stage_three = jnp.einsum('asvqf,vtqr->astrf', stage_two, mpo_ten, precision=prec_mode, preferred_element_type=jnp.float32)
        right_cols = lax.all_to_all(right_rows, 'by', 2, 0, tiled=True)
        part_sum = lax.dot_general(stage_three.reshape(row_share * phys_dim * phys_dim, mpo_dim * col_share), right_cols.reshape(bond_dim, mpo_dim * col_share), (((1,), (1,)), ((), ())), precision=prec_mode, preferred_element_type=jnp.float32)
        part_sum = part_sum.reshape(row_share, phys_dim, phys_dim, bond_dim)
        return lax.psum_scatter(part_sum, 'by', scatter_dimension=3, tiled=True)

    return jax.shard_map(local_apply, mesh=mesh, in_specs=(P('bx', None, None, 'by'), P('bx', None, None), P(), P('by', None, None)), out_specs=P('bx', None, None, 'by'), check_vma=False)
```

profile of v0, /device:TPU:0, one launch (start us, length us, event | category | flops | bytes accessed | tf_op | source)
XLA Modules:
  0.0 276.4 jit_solution(5292334610908685530)
XLA Ops:
  6.5 0.0 copy-start
  6.5 0.0 all-gather.2.cloned.1.call-start
  6.5 0.7 all-gather.2.cloned.1.call-update
  7.3 8.2 %copy.20 = f32[256,5,1024]{0,1,2:T(8,128)} copy(f32[256,5,1024]{2,0,1:T(8,128)} %param.7) | data formatting | bytes 10485760 | tf_op args[3]
  15.5 6.4 %all-to-all-start = ((f32[256,5,1024]{0,1,2:T(8,128)}), f32[256,5,1024]{0,1,2:T(8,128)}, u32[]{:S(2)}, u32[]{:S(2)}) async-start(f32[256,5,1024]{0,1,2:T(8,128)} %copy.20), calls=%async_computation | async-start | bytes 16777216 | tf_op jit(solution)/shard_map/all_to_all | solution.py:19
  21.8 0.0 reduce-scatter.2.cloned.1.call-start
  21.8 26.5 %all-gather.2.cloned.1.call-done = f32[1024,2,2,256]{3,2,1,0:T(2,128)} async-done(((f32[128,2,2,256]{3,2,1,0:T(2,128)}), f32[1024,2,2,256]{3,2,1,0:T(2,128)}) %all-gather.2.cloned.1.call-update) | async-done | bytes 4194320 | tf_op jit(solution)/shard_map/all_gather | solution.py:14
  48.3 7.3 %copy.34 = f32[1024,2,2,256]{0,3,2,1:T(8,128)} copy(f32[1024,2,2,256]{3,2,1,0:T(2,128)} %all-gather.2.cloned.1.call-done) | data formatting | bytes 8388608 | tf_op jit(solution)/shard_map/reshape | solution.py:15
  55.6 0.0 copy-done
  55.6 0.0 copy-start.2
  55.6 10.3 %fusion.12 = f32[128,5,2,2,256,1]{4,0,3,2,1,5:T(8,128)S(1)} fusion(f32[1024,2,2,256]{0,3,2,1:T(8,128)} %copy.34, f32[128,5,1024]{2,0,1:T(8,128)S(1)} %copy-done), kind=kOutput, calls=%fused_computation.10 | convolution fusion | flops 8053063680 | bytes 9437184 | tf_op jit(solution)/shard_map/dot_general | solution.py:15
  65.9 0.0 copy-done.2
  65.9 6.2 %fusion.6 = f32[128,2,256,2,5,1]{2,4,5,1,3,0:T(8,128)S(1)} fusion(f32[128,5,2,2,256,1]{4,0,3,2,1,5:T(8,128)S(1)} %fusion.12, f32[5,2,2,5,1,1]{3,2,1,0,5,4:T(2,128)S(1)} %bitcast.54), kind=kOutput, calls=%fused_computation.6 | convolution fusion | flops 78643200 | bytes 5243280 | tf_op jit(solution)/shard_map/aupqf,uspv->asvqf/dot_general | solution.py:17
  72.1 5.4 %fusion.9 = f32[128,2,2,5,256]{4,3,2,1,0:T(8,128)} fusion(f32[128,2,256,2,5,1]{2,4,5,1,3,0:T(8,128)S(1)} %fusion.6, f32[5,2,2,5,1,1]{3,2,1,0,5,4:T(2,128)S(1)} %bitcast.55), kind=kOutput, calls=%fused_computation.9 | convolution fusion | flops 78643200 | bytes 5243280 | tf_op jit(solution)/shard_map/asvqf,vtqr->astrf/dot_general | solution.py:18
  77.5 4.7 %copy.19 = f32[128,2,2,5,256]{0,4,3,2,1:T(8,128)} copy(f32[128,2,2,5,256]{4,3,2,1,0:T(8,128)} %fusion.9) | data formatting | bytes 5242880 | tf_op jit(solution)/shard_map/asvqf,vtqr->astrf/transpose | solution.py:18
  82.2 123.3 %all-to-all-done = f32[256,5,1024]{0,1,2:T(8,128)} async-done(((f32[256,5,1024]{0,1,2:T(8,128)}), f32[256,5,1024]{0,1,2:T(8,128)}, u32[]{:S(2)}, u32[]{:S(2)}) %all-to-all-start) | async-done | bytes 5242912 | tf_op jit(solution)/shard_map/all_to_all | solution.py:19
  205.5 6.8 %copy.21 = f32[256,5,4,256]{0,2,3,1:T(4,128)S(1)} copy(f32[256,5,4,256]{0,1,3,2:T(8,128)} %bitcast.18) | data formatting | bytes 10485760 | tf_op jit(solution)/shard_map/all_to_all | solution.py:19
  212.2 0.0 copy-start.1
  212.3 1.3 copy.42
  213.6 0.4 copy-done.1
  214.0 9.9 %fusion = f32[128,2,2,1024]{3,0,2,1:T(8,128)} fusion(f32[128,2,2,1280]{0,3,2,1:T(8,128)S(1)} %bitcast.53, f32[1024,1280]{0,1:T(8,128)S(1)} %bitcast.51), kind=kOutput, calls=%fused_computation | convolution fusion | flops 8053063680 | bytes 9961472 | tf_op jit(solution)/shard_map/dot_general | solution.py:20
  223.9 0.0 reduce-scatter.2.cloned.1.call-update
  223.9 43.4 %reduce-scatter.2.cloned.1.call-done = f32[128,2,2,256]{3,0,2,1:T(8,128)} async-done(((f32[128,2,2,1024]{3,0,2,1:T(8,128)}), f32[128,2,2,256]{3,0,2,1:T(8,128)}) %reduce-scatter.2.cloned.1.call-update) | async-done | bytes 524304 | tf_op jit(solution)/shard_map/reduce_scatter | solution.py:22
  267.3 2.2 copy.24
Async XLA Ops:
  6.5 49.1 %copy-start = (f32[128,5,1024]{2,0,1:T(8,128)S(1)}, f32[128,5,1024]{2,0,1:T(8,128)}, u32[]{:S(2)}) copy-start(f32[128,5,1024]{2,0,1:T(8,128)} %param.5) | copy-start | bytes 7864324
  6.5 41.8 %all-gather.2.cloned.1.call-start = ((), (), s32[]{:S(2)}) async-start(), calls=%async_computation.2 | async-start | bytes 4718592 | tf_op jit(solution)/shard_map/all_gather | solution.py:14
  15.5 190.0 %all-to-all-start = ((f32[256,5,1024]{0,1,2:T(8,128)}), f32[256,5,1024]{0,1,2:T(8,128)}, u32[]{:S(2)}, u32[]{:S(2)}) async-start(f32[256,5,1024]{0,1,2:T(8,128)} %copy.20), calls=%async_computation | async-start | bytes 16777216 | tf_op jit(solution)/shard_map/all_to_all | solution.py:19
  21.8 245.5 %reduce-scatter.2.cloned.1.call-start = ((), (), s32[]{:S(2)}) async-start(), calls=%async_computation.3 | async-start | bytes 2621440 | tf_op jit(solution)/shard_map/reduce_scatter | solution.py:22
  55.6 10.3 %copy-start.2 = (f32[5,2,2,5]{3,2,1,0:T(2,128)S(1)}, f32[5,2,2,5]{3,2,1,0:T(2,128)}, u32[]{:S(2)}) copy-start(f32[5,2,2,5]{3,2,1,0:T(2,128)} %param.6) | copy-start | bytes 1204
  212.2 1.7 copy-start.1
Sparse Core Ops, SparseCore 0:
  9.2 39.0 all-gather.1
  224.0 43.2 reduce-scatter.1
where the time goes:
time: 277 us; the launch traced here: 276 us
  waiting for transfers between devices  194 us (70%)
  matrix products  31.7 us (11%)
  local copies, waits for them, and re-layouts  31 us (11%)
  between operations  13.4 us (5%)
  starting transfers between devices  6.38 us (2%)
    all_to_all x1, waiting for transfers between devices, local_apply(): right_cols = lax.all_to_all(right_rows, 'by', 2, 0, tiled=True)  123 us
    reduce_scatter x1, waiting for transfers between devices, local_apply(): return lax.psum_scatter(part_sum, 'by', scatter_dimension=3, tiled=True)  43.4 us
    all_gather x1, waiting for transfers between devices, local_apply(): wave_cols = lax.all_gather(wave_blk, 'bx', axis=0, tiled=True)  26.5 us
    dot_general x1, matrix products, local_apply(): jnp.dot(left_rows.reshape(row_share * mpo_dim, bond_dim), wave_cols.resha...  10.3 us
    unnamed x8, local copies, waits for them, and re-layouts  9.93 us
    dot_general x1, matrix products, local_apply(): lax.dot_general(stage_three.reshape(row_share * phys_dim * phys_dim, mpo_...  9.89 us
    reshape x1, local copies, waits for them, and re-layouts, local_apply(): wave_cols.reshape(bond_dim, phys_dim * phys_dim * col_share)  7.31 us
    all_to_all x1, local copies, waits for them, and re-layouts, local_apply(): right_cols = lax.all_to_all(right_rows, 'by', 2, 0, tiled=True)  6.75 us
  transfers between devices with their start and end apart: 3, of which 3 were waited for; matrix products, arithmetic and copies ran while one was open for 15% of the time, Pallas kernels for 0%

commit v1 on v0

v1 whole, which is shorter than its diff:
```python
import functools

import jax
import jax.numpy as jnp
from jax import lax
from jax.experimental import pallas as pl
from jax.experimental.pallas import tpu as pltpu
from jax.sharding import PartitionSpec as P

MESH = pl.DeviceIdType.MESH
HIGHEST = lax.Precision.HIGHEST
NT = (((1,), (1,)), ((), ()))


def dot_nt(lhs, rhs):
    return lax.dot_general(lhs, rhs, NT, precision=HIGHEST, preferred_element_type=jnp.float32)


def kernel(x_ref, l_ref, w_ref, r_ref, y_ref, xg, rv, acc, vt, lg, pb, ra, rb, rx, ry, rp,
           x_up, x_dn, x_pt, x_in, l_out, l_pt, l_in, loc, s_sem, p_sem, r_sem):
    j, i = lax.axis_index('by'), lax.axis_index('bx')
    chip, core = lax.div(i, 2), lax.rem(i, 2)
    xb, yb = lax.rem(chip, 2), lax.div(chip, 2)
    xc, yc = chip + 1 - 2 * xb, chip + 2 - 4 * yb
    dc = xc + yc - chip
    partner = (j, i + 1 - 2 * core)
    rows = pl.ds(pl.multiple_of(core * 128, 128), 128)
    other_rows = pl.ds(pl.multiple_of((1 - core) * 128, 128), 128)

    def at(chip_, core_):
        return (j, 2 * chip_ + core_)

    def remote(src, dst, send, recv, device):
        return pltpu.make_async_remote_copy(src_ref=src, dst_ref=dst, send_sem=send, recv_sem=recv,
                                            device_id=device, device_id_type=MESH)

    def cols(chip_):
        return pl.ds(pl.multiple_of(chip_ * 256, 256), 256)

    load_r = pltpu.make_async_copy(r_ref.at[:, rows, :], rv, loc.at[0])
    load_x = pltpu.make_async_copy(x_ref, xg.at[j, :, rows, :], loc.at[1])
    load_l = pltpu.make_async_copy(l_ref.at[:, :, cols(chip)], lg.at[i], loc.at[2])
    load_x.start()
    load_r.start()
    load_l.start()

    barrier = pltpu.get_barrier_semaphore()
    near = [partner, at(xc, 0), at(xc, 1), at(yc, 0), at(yc, 1), at(dc, core)]
    for device in near:
        pl.semaphore_signal(barrier, inc=1, device_id=device, device_id_type=MESH)

    @pl.when(j > 0)
    def _():
        pl.semaphore_signal(barrier, inc=1, device_id=(j - 1, i), device_id_type=MESH)

    @pl.when(j < 3)
    def _():
        pl.semaphore_signal(barrier, inc=1, device_id=(j + 1, i), device_id_type=MESH)

    @pl.when((j > 0) & (j < 3))
    def _():
        pl.semaphore_wait(barrier, 8)

    @pl.when((j == 0) | (j == 3))
    def _():
        pl.semaphore_wait(barrier, 7)

    def x_copy(src, z, q, sems, device):
        return remote(src, xg.at[z, q, rows, :], sems.at[z, q], x_in.at[z, q, core], device)

    def x_held(z, q):
        return xg.at[z, q, rows, :]

    for q in range(4):
        @pl.when(j < 3)
        def _():
            x_copy(x_ref.at[q], j, q, x_up, (j + 1, i)).start()

        @pl.when(j > 0)
        def _():
            x_copy(x_ref.at[q], j, q, x_dn, (j - 1, i)).start()

        x_copy(x_ref.at[q], j, q, x_pt, partner).start()

    def l_copy(chip_, n):
        return remote(l_ref.at[:, :, cols(chip_)], lg.at[i], l_out.at[n], l_in.at[i], at(chip_, core))

    def l_pass(chip_, n):
        slot = 2 * chip_ + core
        return remote(lg.at[slot], lg.at[slot], l_pt.at[n], l_in.at[slot], partner)

    for n, chip_ in enumerate((xc, yc, dc)):
        l_copy(chip_, n).start()
    load_l.wait()
    l_pass(chip, 3).start()
    load_x.wait()
    load_r.wait()

    def arrive(z, q):
        x_copy(x_held(z, q), z, q, x_pt, partner).wait_recv()

    low = j < 2
    jm = jnp.where(low, j, 3 - j)

    def step(n, _):
        t, q = lax.div(n, 4), lax.rem(n, 4)

        @pl.when((t > 0) & (n < 16) & (j - t >= 0))
        def _():
            z = j - t
            arrive(z, q)

            @pl.when(j < 3)
            def _():
                x_copy(x_held(z, q), z, q, x_up, (j + 1, i)).start()

            x_copy(x_held(z, q), z, q, x_pt, partner).start()

        @pl.when((t > 0) & (n < 16) & (j + t <= 3))
        def _():
            z = j + t
            arrive(z, q)

            @pl.when(j > 0)
            def _():
                x_copy(x_held(z, q), z, q, x_dn, (j - 1, i)).start()

            x_copy(x_held(z, q), z, q, x_pt, partner).start()

        @pl.when(n == 12)
        def _():
            for m, chip_ in enumerate((xc, yc)):
                l_pass(chip_, m).wait_recv()
                l_pass(chip_, m).start()

        @pl.when(n == 15)
        def _():
            l_pass(dc, 2).wait_recv()
            l_pass(dc, 2).start()

        @pl.when(n > 0)
        def _():
            tt, qq = lax.div(n - 1, 4), lax.rem(n - 1, 4)
            zm = jnp.where(tt == 0, jm, jnp.where(tt == 1, 1 - jm, tt))
            z = jnp.where(low, zm, 3 - zm)
            remote(xg.at[z, qq, other_rows, :], xg.at[z, qq, other_rows, :], x_pt.at[z, qq],
                   x_in.at[z, qq, 1 - core], partner).wait_recv()
            lhs = rv[:, :, pl.ds(pl.multiple_of(z * 256, 256), 256)].reshape(640, 256)
            part = dot_nt(lhs, xg[z, qq]).reshape(5, 128, 256)
            dst = acc.at[:, :, pl.ds(pl.multiple_of(qq * 256, 256), 256)]

            @pl.when(tt == 0)
            def _():
                dst[...] = part

            @pl.when(tt > 0)
            def _():
                dst[...] += part

        return 0

    lax.fori_loop(0, 17, step, 0)

    def wt(u, s, p, v):
        return w_ref[((u * 2 + s) * 2 + p) * 5 + v]

    def sites(t):
        def tile(n, _):
            b = pl.ds(pl.multiple_of(n * 8, 8), 8)
            mid = []
            for p in range(2):
                parts = [acc[r, b, (p * 2 + q) * 256:(p * 2 + q + 1) * 256] for q in range(2) for r in range(5)]
                for v in range(5):
                    tot = None
                    for q in range(2):
                        for r in range(5):
                            term = parts[q * 5 + r] * wt(v, t, q, r)
                            tot = term if tot is None else tot + term
                    mid.append(tot)
            for u in range(5):
                for s in range(2):
                    tot = None
                    for p in range(2):
                        for v in range(5):
                            term = mid[p * 5 + v] * wt(u, s, p, v)
                            tot = term if tot is None else tot + term
                    vt[t, pl.ds(pl.multiple_of(s * 128 + n * 8, 8), 8), u * 256:(u + 1) * 256] = tot
            return 0

        lax.fori_loop(0, 16, tile, 0)

    def left(slots, t):
        lhs = jnp.concatenate(
            [jnp.concatenate([lg[slot, u] for u in range(5)], axis=1) for slot in slots], axis=0)
        return dot_nt(lhs, vt[t])

    def wait_left(chip_):
        slot = 2 * chip_ + 1 - core
        remote(lg.at[slot], lg.at[slot], l_pt.at[0], l_in.at[slot], partner).wait_recv()

    def send_far(h, t):
        if h == 0:
            return remote(pb.at[0, t], ra.at[t], s_sem.at[0, t], p_sem.at[0, t], at(xc, core))
        return remote(pb.at[1, t], rb.at[t], s_sem.at[1, t], p_sem.at[1, t], at(yc, core))

    def send_x(n, h, t):
        return remote(pb.at[n, t], rx.at[core, t], s_sem.at[n, t], r_sem.at[0, core, t], at(xc, h))

    def send_y(n, h, t):
        return remote(pb.at[n, t], ry.at[core, t], s_sem.at[n, t], r_sem.at[1, core, t], at(yc, h))

    def send_pt(t):
        return remote(pb.at[6, t], rp.at[t], s_sem.at[6, t], p_sem.at[2, t], partner)

    wait_left(dc)
    for t in range(2):
        sites(t)
        res = left((2 * dc, 2 * dc + 1), t)
        pb[0, t] = res[:128]
        pb[1, t] = res[128:]
        send_far(0, t).start()
        send_far(1, t).start()
    wait_left(xc)
    wait_left(yc)
    for t in range(2):
        res = left((2 * xc, 2 * yc + 1), t)
        pb[2, t] = res[:128]
        pb[3, t] = res[128:]
        send_x(2, 0, t).start()
        send_y(3, 1, t).start()
    for t in range(2):
        res = left((2 * yc, 2 * xc + 1), t)
        send_far(0, t).wait_recv()
        send_far(1, t).wait_recv()
        pb[4, t] = res[:128] + ra[t]
        pb[5, t] = res[128:] + rb[t]
        send_y(4, 0, t).start()
        send_x(5, 1, t).start()
    wait_left(chip)
    for t in range(2):
        res = left((2 * chip + 1 - core, 2 * chip + core), t)
        pb[6, t] = res[:128]
        pb[7, t] = res[128:]
        send_pt(t).start()
    for t in range(2):
        send_pt(t).wait_recv()
        for half in range(2):
            remote(rx.at[half, t], rx.at[half, t], s_sem.at[0, t], r_sem.at[0, half, t], partner).wait_recv()
            remote(ry.at[half, t], ry.at[half, t], s_sem.at[0, t], r_sem.at[1, half, t], partner).wait_recv()
        for s in range(2):
            lanes = slice(s * 128, (s + 1) * 128)
            y_ref[s * 2 + t, :, rows] = pb[7, t, :, lanes] + (rx[core, t, :, lanes] + ry[core, t, :, lanes])
            y_ref[s * 2 + t, :, other_rows] = rp[t, :, lanes] + (rx[1 - core, t, :, lanes] + ry[1 - core, t, :, lanes])

    def drain(n, _):
        z, q = lax.div(n, 4), lax.rem(n, 4)

        @pl.when((z <= j) & (j < 3))
        def _():
            x_copy(x_held(z, q), z, q, x_up, (j + 1, i)).wait_send()

        @pl.when((z >= j) & (j > 0))
        def _():
            x_copy(x_held(z, q), z, q, x_dn, (j - 1, i)).wait_send()

        x_copy(x_held(z, q), z, q, x_pt, partner).wait_send()
        return 0

    lax.fori_loop(0, 16, drain, 0)
    for n, chip_ in enumerate((xc, yc, dc)):
        l_copy(chip_, n).wait_send()
        l_pass(chip_, n).wait_send()
    l_pass(chip, 3).wait_send()
    for t in range(2):
        send_far(0, t).wait_send()
        send_far(1, t).wait_send()
        send_x(2, 0, t).wait_send()
        send_y(3, 1, t).wait_send()
        send_y(4, 0, t).wait_send()
        send_x(5, 1, t).wait_send()
        send_pt(t).wait_send()


def solution(mesh):
    def local_apply(wave, left, mpo, right):
        x = wave.reshape(128, 4, 256).transpose(1, 0, 2)
        f32, vmem, sem = jnp.float32, pltpu.VMEM, pltpu.SemaphoreType.DMA
        y = pl.pallas_call(
            kernel,
            out_shape=jax.ShapeDtypeStruct((4, 128, 256), f32),
            in_specs=[pl.BlockSpec(memory_space=pl.ANY), pl.BlockSpec(memory_space=pl.ANY),
                      pl.BlockSpec(memory_space=pltpu.SMEM), pl.BlockSpec(memory_space=pl.ANY)],
            out_specs=pl.BlockSpec(memory_space=pltpu.VMEM),
            scratch_shapes=[
                vmem((4, 4, 256, 256), f32), vmem((5, 128, 1024), f32), vmem((5, 128, 1024), f32),
                vmem((2, 256, 1280), f32), vmem((8, 5, 128, 256), f32), vmem((8, 2, 128, 256), f32),
                vmem((2, 128, 256), f32), vmem((2, 128, 256), f32), vmem((2, 2, 128, 256), f32),
                vmem((2, 2, 128, 256), f32), vmem((2, 128, 256), f32),
                sem((4, 4)), sem((4, 4)), sem((4, 4)), sem((4, 4, 2)), sem((3,)), sem((4,)), sem((8,)), sem((3,)),
                sem((7, 2)), sem((3, 2)), sem((2, 2, 2)),
            ],
            compiler_params=pltpu.CompilerParams(collective_id=0, has_side_effects=True,
                                                 vmem_limit_bytes=48 * 1024 * 1024),
        )(x, left.transpose(1, 0, 2), mpo.reshape(100), right.transpose(1, 0, 2))
        return y.reshape(2, 2, 128, 256).transpose(2, 0, 1, 3)

    return jax.shard_map(local_apply, mesh=mesh,
                         in_specs=(P('bx', None, None, 'by'), P('bx', None, None), P(), P('by', None, None)),
                         out_specs=P('bx', None, None, 'by'), check_vma=False)
```

time: 277 us -> 73.9 us (0.27)
  waiting for transfers between devices: 194 us -> 0 us
  Pallas kernels: 0 us -> 68.8 us
  matrix products: 31.7 us -> 0 us
  local copies, waits for them, and re-layouts: 31 us -> 4.88 us
  between operations: 13.4 us -> 0.02 us
  starting transfers between devices: 6.38 us -> 0 us
    all_to_all x1 -> x0, waiting for transfers between devices: 123 us -> none  [local_apply(): right_cols = lax.all_to_all(right_rows, 'by', 2, 0, tiled=True)]
    pallas_call x0 -> x1, Pallas kernels: none -> 68.8 us  [local_apply(): pl.pallas_call(kernel, out_shape=jax.ShapeDtypeStruct((4, 128, 256), f32)...]
    reduce_scatter x1 -> x0, waiting for transfers between devices: 43.4 us -> none  [local_apply(): return lax.psum_scatter(part_sum, 'by', scatter_dimension=3, tiled=True)]
    dot_general x4 -> x0, matrix products: 31.7 us -> none  [the longest x1 10.3 us: local_apply(): jnp.dot(left_rows.reshape(row_share * mpo_dim, bond_dim), wave_cols.resha...]
    all_gather x1 -> x0, waiting for transfers between devices: 26.5 us -> none  [local_apply(): wave_cols = lax.all_gather(wave_blk, 'bx', axis=0, tiled=True)]
    unnamed x8 -> x3, local copies, waits for them, and re-layouts: 9.93 us -> 2.88 us
    all_to_all x1 -> x0, local copies, waits for them, and re-layouts: 6.75 us -> none  [local_apply(): right_cols = lax.all_to_all(right_rows, 'by', 2, 0, tiled=True)]
    all_to_all x1 -> x0, starting transfers between devices: 6.38 us -> none  [local_apply(): right_cols = lax.all_to_all(right_rows, 'by', 2, 0, tiled=True)]
  transfers between devices with their start and end apart: 3 -> 0, of which waited for: 3 -> 0; matrix products, arithmetic and copies ran while one was open for 15% -> 0% of each run, Pallas kernels for 0% -> 0%
where the time goes in v1:
time: 73.9 us; the launch traced here: 73.7 us
  Pallas kernels  68.8 us (93%)
  local copies, waits for them, and re-layouts  4.88 us (7%)
    pallas_call x1, Pallas kernels, local_apply(): pl.pallas_call(kernel, out_shape=jax.ShapeDtypeStruct((4, 128, 256), f32)...  68.8 us
    unnamed x3, local copies, waits for them, and re-layouts  2.88 us

profile of v1, /device:TPU:0, one launch (start us, length us, event | category | flops | bytes accessed | tf_op | source)
XLA Modules:
  0.0 73.7 jit_solution(17121438269922173545)
XLA Ops:
  0.0 0.8 %reshape.10.w_ref = f32[100]{0:T(128)S(1)} reshape(f32[5,2,2,5]{3,2,1,0:T(2,128)} %param.6) | data formatting | bytes 800 | tf_op jit(solution)/shard_map/reshape | solution.py:304
  0.8 1.1 %copy.5 = f32[128,2,2,256]{3,0,2,1:T(8,128)S(1)} copy(f32[128,2,2,256]{3,2,1,0:T(2,128)} %param.4) | data formatting | bytes 1048576 | tf_op args[0]
  1.9 0.0 copy-start
  2.0 1.7 %copy-done = f32[128,5,1024]{2,0,1:T(8,128)S(1)} copy-done((f32[128,5,1024]{2,0,1:T(8,128)S(1)}, f32[128,5,1024]{2,0,1:T(8,128)}, u32[]{:S(2)}) %copy-start) | copy-done | bytes 2621464
  3.7 68.8 %shard_map.46 = f32[4,128,256]{2,1,0:T(8,128)S(1)} custom-call(f32[4,128,256]{2,1,0:T(8,128)S(1)} %bitcast.11, f32[5,128,1024]{2,1,0:T(8,128)S(1)} %bitcast.9, f32[100]{0:T(128)S(1)} %reshape.10.w_ref, f32[5,256,1024]{2,1,0:T(8,128)} %bitcast.12), custom_call_target="tpu_custom_call" | custom-call | tf_op jit(solution)/shard_map/pallas_call | solution.py:288
  72.5 1.2 %copy.8 = f32[2,2,128,256]{3,1,0,2:T(2,128)} copy(f32[2,2,128,256]{3,2,1,0:T(8,128)S(1)} %bitcast.10) | data formatting | bytes 1048576 | tf_op jit(solution)/shard_map/reshape | solution.py:305
Async XLA Ops:
  1.9 1.7 %copy-start = (f32[128,5,1024]{2,0,1:T(8,128)S(1)}, f32[128,5,1024]{2,0,1:T(8,128)}, u32[]{:S(2)}) copy-start(f32[128,5,1024]{2,0,1:T(8,128)} %param.5) | copy-start | bytes 7864324

commit v2 on v1

--- a/solution.py
+++ b/solution.py
@@ -16,7 +16,7 @@
     return lax.dot_general(lhs, rhs, NT, precision=HIGHEST, preferred_element_type=jnp.float32)
 
 
-def kernel(x_ref, l_ref, w_ref, r_ref, y_ref, xg, rv, acc, vt, lg, pb, ra, rb, rx, ry, rp,
+def kernel(x_ref, l_ref, w_hbm, r_ref, y_ref, xv, w_ref, xg, rv, acc, vt, lg, pb, ra, rb, rx, ry, rp,
            x_up, x_dn, x_pt, x_in, l_out, l_pt, l_in, loc, s_sem, p_sem, r_sem):
     j, i = lax.axis_index('by'), lax.axis_index('bx')
     chip, core = lax.div(i, 2), lax.rem(i, 2)
@@ -38,9 +38,11 @@
         return pl.ds(pl.multiple_of(chip_ * 256, 256), 256)
 
     load_r = pltpu.make_async_copy(r_ref.at[:, rows, :], rv, loc.at[0])
-    load_x = pltpu.make_async_copy(x_ref, xg.at[j, :, rows, :], loc.at[1])
+    load_x = pltpu.make_async_copy(x_ref, xv, loc.at[1])
+    load_w = pltpu.make_async_copy(w_hbm, w_ref, loc.at[3])
     load_l = pltpu.make_async_copy(l_ref.at[:, :, cols(chip)], lg.at[i], loc.at[2])
     load_x.start()
+    load_w.start()
     load_r.start()
     load_l.start()
 
@@ -57,6 +59,12 @@
     def _():
         pl.semaphore_signal(barrier, inc=1, device_id=(j + 1, i), device_id_type=MESH)
 
+    load_x.wait()
+    for p in range(2):
+        for half in range(2):
+            for q in range(2):
+                xg[j, p * 2 + q, rows, half * 128:(half + 1) * 128] = xv[pl.ds(p * 4 + half * 2 + q, 128, stride=8), :]
+
     @pl.when((j > 0) & (j < 3))
     def _():
         pl.semaphore_wait(barrier, 8)
@@ -74,13 +82,13 @@
     for q in range(4):
         @pl.when(j < 3)
         def _():
-            x_copy(x_ref.at[q], j, q, x_up, (j + 1, i)).start()
+            x_copy(x_held(j, q), j, q, x_up, (j + 1, i)).start()
 
         @pl.when(j > 0)
         def _():
-            x_copy(x_ref.at[q], j, q, x_dn, (j - 1, i)).start()
-
-        x_copy(x_ref.at[q], j, q, x_pt, partner).start()
+            x_copy(x_held(j, q), j, q, x_dn, (j - 1, i)).start()
+
+        x_copy(x_held(j, q), j, q, x_pt, partner).start()
 
     def l_copy(chip_, n):
         return remote(l_ref.at[:, :, cols(chip_)], lg.at[i], l_out.at[n], l_in.at[i], at(chip_, core))
@@ -93,7 +101,7 @@
         l_copy(chip_, n).start()
     load_l.wait()
     l_pass(chip, 3).start()
-    load_x.wait()
+    load_w.wait()
     load_r.wait()
 
     def arrive(z, q):
@@ -162,7 +170,7 @@
     lax.fori_loop(0, 17, step, 0)
 
     def wt(u, s, p, v):
-        return w_ref[((u * 2 + s) * 2 + p) * 5 + v]
+        return w_ref[u, s, p, v]
 
     def sites(t):
         def tile(n, _):
@@ -249,8 +257,10 @@
             remote(ry.at[half, t], ry.at[half, t], s_sem.at[0, t], r_sem.at[1, half, t], partner).wait_recv()
         for s in range(2):
             lanes = slice(s * 128, (s + 1) * 128)
-            y_ref[s * 2 + t, :, rows] = pb[7, t, :, lanes] + (rx[core, t, :, lanes] + ry[core, t, :, lanes])
-            y_ref[s * 2 + t, :, other_rows] = rp[t, :, lanes] + (rx[1 - core, t, :, lanes] + ry[1 - core, t, :, lanes])
+            y_ref[pl.ds(s * 4 + core * 2 + t, 128, stride=8), :] = (
+                pb[7, t, :, lanes] + (rx[core, t, :, lanes] + ry[core, t, :, lanes]))
+            y_ref[pl.ds(s * 4 + (1 - core) * 2 + t, 128, stride=8), :] = (
+                rp[t, :, lanes] + (rx[1 - core, t, :, lanes] + ry[1 - core, t, :, lanes]))
 
     def drain(n, _):
         z, q = lax.div(n, 4), lax.rem(n, 4)
@@ -283,26 +293,27 @@
 
 def solution(mesh):
     def local_apply(wave, left, mpo, right):
-        x = wave.reshape(128, 4, 256).transpose(1, 0, 2)
+        x = wave.reshape(128, 2, 2, 2, 128).transpose(0, 1, 3, 2, 4).reshape(1024, 128)
         f32, vmem, sem = jnp.float32, pltpu.VMEM, pltpu.SemaphoreType.DMA
         y = pl.pallas_call(
             kernel,
-            out_shape=jax.ShapeDtypeStruct((4, 128, 256), f32),
-            in_specs=[pl.BlockSpec(memory_space=pl.ANY), pl.BlockSpec(memory_space=pl.ANY),
-                      pl.BlockSpec(memory_space=pltpu.SMEM), pl.BlockSpec(memory_space=pl.ANY)],
+            out_shape=jax.ShapeDtypeStruct((1024, 128), f32),
+            in_specs=[pl.BlockSpec(memory_space=pltpu.HBM), pl.BlockSpec(memory_space=pltpu.HBM),
+                      pl.BlockSpec(memory_space=pltpu.HBM), pl.BlockSpec(memory_space=pltpu.HBM)],
             out_specs=pl.BlockSpec(memory_space=pltpu.VMEM),
             scratch_shapes=[
+                vmem((1024, 128), f32), pltpu.SMEM((5, 2, 2, 5), f32),
                 vmem((4, 4, 256, 256), f32), vmem((5, 128, 1024), f32), vmem((5, 128, 1024), f32),
                 vmem((2, 256, 1280), f32), vmem((8, 5, 128, 256), f32), vmem((8, 2, 128, 256), f32),
                 vmem((2, 128, 256), f32), vmem((2, 128, 256), f32), vmem((2, 2, 128, 256), f32),
                 vmem((2, 2, 128, 256), f32), vmem((2, 128, 256), f32),
-                sem((4, 4)), sem((4, 4)), sem((4, 4)), sem((4, 4, 2)), sem((3,)), sem((4,)), sem((8,)), sem((3,)),
+                sem((4, 4)), sem((4, 4)), sem((4, 4)), sem((4, 4, 2)), sem((3,)), sem((4,)), sem((8,)), sem((4,)),
                 sem((7, 2)), sem((3, 2)), sem((2, 2, 2)),
             ],
             compiler_params=pltpu.CompilerParams(collective_id=0, has_side_effects=True,
-                                                 vmem_limit_bytes=48 * 1024 * 1024),
-        )(x, left.transpose(1, 0, 2), mpo.reshape(100), right.transpose(1, 0, 2))
-        return y.reshape(2, 2, 128, 256).transpose(2, 0, 1, 3)
+                                                 vmem_limit_bytes=53 * 1024 * 1024),
+        )(x, left.transpose(1, 0, 2), mpo, right.transpose(1, 0, 2))
+        return y.reshape(128, 2, 2, 2, 128).transpose(0, 1, 3, 2, 4).reshape(128, 2, 2, 256)
 
     return jax.shard_map(local_apply, mesh=mesh,
                          in_specs=(P('bx', None, None, 'by'), P('bx', None, None), P(), P('by', None, None)),

time: 73.9 us -> 69.8 us (0.945)
  local copies, waits for them, and re-layouts: 4.88 us -> 1.5 us
    reshape x2 -> x0, local copies, waits for them, and re-layouts: 1.99 us -> none  [the longest x1 1.2 us: local_apply(): return y.reshape(2, 2, 128, 256).transpose(2, 0, 1, 3)]
    unnamed x3, local copies, waits for them, and re-layouts: 2.88 us -> 1.5 us
where the time goes in v2:
time: 69.8 us; the launch traced here: 69.6 us
  Pallas kernels  68.1 us (98%)
  local copies, waits for them, and re-layouts  1.5 us (2%)
    pallas_call x1, Pallas kernels, local_apply(): pl.pallas_call(kernel, out_shape=jax.ShapeDtypeStruct((1024, 128), f32),...  68.1 us
    unnamed x3, local copies, waits for them, and re-layouts  1.5 us

profile of v2, /device:TPU:0, one launch (start us, length us, event | category | flops | bytes accessed | tf_op | source)
XLA Modules:
  0.0 69.6 jit_solution(6483037280725704504)
XLA Ops:
  0.0 0.0 copy-start
  0.0 0.7 %copy-done = f32[5,2,2,5]{3,2,1,0:T(2,128)S(1)} copy-done((f32[5,2,2,5]{3,2,1,0:T(2,128)S(1)}, f32[5,2,2,5]{3,2,1,0:T(2,128)}, u32[]{:S(2)}) %copy-start) | copy-done | bytes 424
  0.7 68.1 %shard_map.46 = f32[1024,128]{1,0:T(8,128)S(1)} custom-call(f32[1024,128]{1,0:T(8,128)} %bitcast.15, f32[5,128,1024]{2,1,0:T(8,128)} %bitcast.14, f32[5,2,2,5]{3,2,1,0:T(2,128)S(1)} %copy-done, f32[5,256,1024]{2,1,0:T(8,128)} %bitcast.13), custom_call_target="tpu_custom_call" | custom-call | tf_op jit(solution)/shard_map/pallas_call | solution.py:298
  68.8 0.8 %copy.8 = f32[128,2,2,256]{3,2,1,0:T(2,128)} copy(f32[128,2,2,256]{3,2,1,0:T(2,128)S(1)} %bitcast.12) | data formatting | bytes 1048576
Async XLA Ops:
  0.0 0.7 %copy-start = (f32[5,2,2,5]{3,2,1,0:T(2,128)S(1)}, f32[5,2,2,5]{3,2,1,0:T(2,128)}, u32[]{:S(2)}) copy-start(f32[5,2,2,5]{3,2,1,0:T(2,128)} %w_hbm.1) | copy-start | bytes 1204

commit v3 on v2

--- a/solution.py
+++ b/solution.py
@@ -16,8 +16,8 @@
     return lax.dot_general(lhs, rhs, NT, precision=HIGHEST, preferred_element_type=jnp.float32)
 
 
-def kernel(x_ref, l_ref, w_hbm, r_ref, y_ref, xv, w_ref, xg, rv, acc, vt, lg, pb, ra, rb, rx, ry, rp,
-           x_up, x_dn, x_pt, x_in, l_out, l_pt, l_in, loc, s_sem, p_sem, r_sem):
+def kernel(x_ref, l_ref, w_hbm, r_ref, y_ref, xv, w_ref, xg, rv, acc, zp, vt, lg, pb, ra, rb, rx, ry, rp,
+           x_up, x_dn, x_pt, x_in, l_out, l_pt, l_in, loc, s_sem, p_sem, r_sem, rq, q_out, q_in):
     j, i = lax.axis_index('by'), lax.axis_index('bx')
     chip, core = lax.div(i, 2), lax.rem(i, 2)
     xb, yb = lax.rem(chip, 2), lax.div(chip, 2)
@@ -47,7 +47,10 @@
     load_l.start()
 
     barrier = pltpu.get_barrier_semaphore()
-    near = [partner, at(xc, 0), at(xc, 1), at(yc, 0), at(yc, 1), at(dc, core)]
+    end = (j == 0) | (j == 3)
+    pair = j + 1 - 2 * lax.rem(j, 2)
+    near = [partner, at(xc, 0), at(xc, 1), at(yc, 0), at(yc, 1), at(dc, core),
+            (pair, 2 * xc + core), (pair, 2 * yc + core), (pair, 2 * chip + 1 - core)]
     for device in near:
         pl.semaphore_signal(barrier, inc=1, device_id=device, device_id_type=MESH)
 
@@ -67,11 +70,11 @@
 
     @pl.when((j > 0) & (j < 3))
     def _():
-        pl.semaphore_wait(barrier, 8)
+        pl.semaphore_wait(barrier, 11)
 
     @pl.when((j == 0) | (j == 3))
     def _():
-        pl.semaphore_wait(barrier, 7)
+        pl.semaphore_wait(barrier, 10)
 
     def x_copy(src, z, q, sems, device):
         return remote(src, xg.at[z, q, rows, :], sems.at[z, q], x_in.at[z, q, core], device)
@@ -106,6 +109,51 @@
 
     def arrive(z, q):
         x_copy(x_held(z, q), z, q, x_pt, partner).wait_recv()
+
+    def wt(u, s, p, v):
+        return w_ref[u, s, p, v]
+
+    def field(r, p, q, b):
+        return acc[r, b, (p * 2 + q) * 256:(p * 2 + q + 1) * 256]
+
+    def dots(terms):
+        total = None
+        for weight, value in terms:
+            total = value * weight if total is None else total + value * weight
+        return total
+
+    def tiles(body):
+        def tile(n, _):
+            body(pl.ds(pl.multiple_of(n * 8, 8), 8), n * 8)
+            return 0
+
+        lax.fori_loop(0, 16, tile, 0)
+
+    def sites_first(b, start):
+        parts = [(q, r, field(r, 0, q, b)) for q in range(2) for r in range(5)]
+        for t in range(2):
+            mid = [dots((wt(v, t, q, r), x) for q, r, x in parts) for v in range(5)]
+            for s in range(2):
+                into = pl.ds(pl.multiple_of(s * 128 + start, 8), 8)
+                for u in range(5):
+                    vt[t, into, u * 256:(u + 1) * 256] = dots((wt(u, s, 0, v), mid[v]) for v in range(5))
+
+    def sites_second(b, start):
+        parts = [field(r, 1, 0, b) for r in range(5)]
+        for t in range(2):
+            for v in range(5):
+                zp[t, v, b, :] = dots((wt(v, t, 0, r), parts[r]) for r in range(5))
+
+    def sites_last(t):
+        def body(b, start):
+            parts = [field(r, 1, 1, b) for r in range(5)]
+            mid = [zp[t, v, b, :] + dots((wt(v, t, 1, r), parts[r]) for r in range(5)) for v in range(5)]
+            for s in range(2):
+                into = pl.ds(pl.multiple_of(s * 128 + start, 8), 8)
+                for u in range(5):
+                    vt[t, into, u * 256:(u + 1) * 256] += dots((wt(u, s, 1, v), mid[v]) for v in range(5))
+
+        tiles(body)
 
     low = j < 2
     jm = jnp.where(low, j, 3 - j)
@@ -165,41 +213,21 @@
             def _():
                 dst[...] += part
 
+        @pl.when(n == 14)
+        def _():
+            tiles(sites_first)
+
+        @pl.when(n == 15)
+        def _():
+            tiles(sites_second)
+
         return 0
 
     lax.fori_loop(0, 17, step, 0)
 
-    def wt(u, s, p, v):
-        return w_ref[u, s, p, v]
-
-    def sites(t):
-        def tile(n, _):
-            b = pl.ds(pl.multiple_of(n * 8, 8), 8)
-            mid = []
-            for p in range(2):
-                parts = [acc[r, b, (p * 2 + q) * 256:(p * 2 + q + 1) * 256] for q in range(2) for r in range(5)]
-                for v in range(5):
-                    tot = None
-                    for q in range(2):
-                        for r in range(5):
-                            term = parts[q * 5 + r] * wt(v, t, q, r)
-                            tot = term if tot is None else tot + term
-                    mid.append(tot)
-            for u in range(5):
-                for s in range(2):
-                    tot = None
-                    for p in range(2):
-                        for v in range(5):
-                            term = mid[p * 5 + v] * wt(u, s, p, v)
-                            tot = term if tot is None else tot + term
-                    vt[t, pl.ds(pl.multiple_of(s * 128 + n * 8, 8), 8), u * 256:(u + 1) * 256] = tot
-            return 0
-
-        lax.fori_loop(0, 16, tile, 0)
-
-    def left(slots, t):
+    def left(first, second, t):
         lhs = jnp.concatenate(
-            [jnp.concatenate([lg[slot, u] for u in range(5)], axis=1) for slot in slots], axis=0)
+            [jnp.concatenate([lg[slot, u] for u in range(5)], axis=1) for slot in (first, second)], axis=0)
         return dot_nt(lhs, vt[t])
 
     def wait_left(chip_):
@@ -220,36 +248,95 @@
     def send_pt(t):
         return remote(pb.at[6, t], rp.at[t], s_sem.at[6, t], p_sem.at[2, t], partner)
 
+    def send_via(h):
+        return remote(pb.at[2 + h, 0], rq.at[h], s_sem.at[2 + h, 0], q_in.at[h], (pair, 2 * (yc if h else xc) + core))
+
+    def send_back(h):
+        land = ry if h else rx
+        return remote(rq.at[h], land.at[core, 0], q_out.at[h], r_sem.at[h, core, 0], (pair, 2 * chip + h))
+
     wait_left(dc)
-    for t in range(2):
-        sites(t)
-        res = left((2 * dc, 2 * dc + 1), t)
-        pb[0, t] = res[:128]
-        pb[1, t] = res[128:]
-        send_far(0, t).start()
-        send_far(1, t).start()
     wait_left(xc)
     wait_left(yc)
-    for t in range(2):
-        res = left((2 * xc, 2 * yc + 1), t)
-        pb[2, t] = res[:128]
-        pb[3, t] = res[128:]
-        send_x(2, 0, t).start()
-        send_y(3, 1, t).start()
-    for t in range(2):
-        res = left((2 * yc, 2 * xc + 1), t)
-        send_far(0, t).wait_recv()
-        send_far(1, t).wait_recv()
-        pb[4, t] = res[:128] + ra[t]
-        pb[5, t] = res[128:] + rb[t]
-        send_y(4, 0, t).start()
-        send_x(5, 1, t).start()
     wait_left(chip)
-    for t in range(2):
-        res = left((2 * chip + 1 - core, 2 * chip + core), t)
-        pb[6, t] = res[:128]
-        pb[7, t] = res[128:]
-        send_pt(t).start()
+
+    def stage(n, _):
+        role = jnp.where(n < 4, lax.rem(n, 2), jnp.where((n == 4) | (n == 7), 3, 2))
+        t = jnp.where(n < 4, lax.div(n, 2), lax.div(n - 4, 2))
+
+        @pl.when((n == 0) | (n == 2))
+        def _():
+            sites_last(t)
+
+        def pick(far, near, via, own):
+            return jnp.where(role == 0, far, jnp.where(role == 1, near, jnp.where(role == 2, via, own)))
+
+        first = pick(2 * dc, 2 * xc, 2 * yc, 2 * chip + 1 - core)
+        second = pick(2 * dc + 1, 2 * yc + 1, 2 * xc + 1, 2 * chip + core)
+        res = left(first, second, t)
+
+        @pl.when(role != 2)
+        def _():
+            pb[2 * role, t] = res[:128]
+            pb[2 * role + 1, t] = res[128:]
+
+        @pl.when((n == 6) & jnp.logical_not(end))
+        def _():
+            for h in range(2):
+                send_via(h).wait_recv()
+                send_back(h).start()
+
+        @pl.when(role == 2)
+        def _():
+            send_far(0, t).wait_recv()
+            send_far(1, t).wait_recv()
+            pb[4, t] = res[:128] + ra[t]
+            pb[5, t] = res[128:] + rb[t]
+            send_y(4, 0, t).start()
+            send_x(5, 1, t).start()
+
+        @pl.when(role == 0)
+        def _():
+            send_far(0, t).start()
+            send_far(1, t).start()
+
+        @pl.when((role == 1) & (end & (t == 0)))
+        def _():
+            send_via(0).start()
+            send_via(1).start()
+
+        @pl.when((role == 1) & jnp.logical_not(end & (t == 0)))
+        def _():
+            send_x(2, 0, t).start()
+            send_y(3, 1, t).start()
+
+        @pl.when(role == 3)
+        def _():
+            send_pt(t).start()
+
+        return 0
+
+    lax.fori_loop(0, 8, stage, 0)
+
+    def drain(n, _):
+        z, q = lax.div(n, 4), lax.rem(n, 4)
+
+        @pl.when((z <= j) & (j < 3))
+        def _():
+            x_copy(x_held(z, q), z, q, x_up, (j + 1, i)).wait_send()
+
+        @pl.when((z >= j) & (j > 0))
+        def _():
+            x_copy(x_held(z, q), z, q, x_dn, (j - 1, i)).wait_send()
+
+        x_copy(x_held(z, q), z, q, x_pt, partner).wait_send()
+        return 0
+
+    lax.fori_loop(0, 16, drain, 0)
+    for n, chip_ in enumerate((xc, yc, dc)):
+        l_copy(chip_, n).wait_send()
+        l_pass(chip_, n).wait_send()
+    l_pass(chip, 3).wait_send()
     for t in range(2):
         send_pt(t).wait_recv()
         for half in range(2):
@@ -262,25 +349,11 @@
             y_ref[pl.ds(s * 4 + (1 - core) * 2 + t, 128, stride=8), :] = (
                 rp[t, :, lanes] + (rx[1 - core, t, :, lanes] + ry[1 - core, t, :, lanes]))
 
-    def drain(n, _):
-        z, q = lax.div(n, 4), lax.rem(n, 4)
-
-        @pl.when((z <= j) & (j < 3))
-        def _():
-            x_copy(x_held(z, q), z, q, x_up, (j + 1, i)).wait_send()
-
-        @pl.when((z >= j) & (j > 0))
-        def _():
-            x_copy(x_held(z, q), z, q, x_dn, (j - 1, i)).wait_send()
-
-        x_copy(x_held(z, q), z, q, x_pt, partner).wait_send()
-        return 0
-
-    lax.fori_loop(0, 16, drain, 0)
-    for n, chip_ in enumerate((xc, yc, dc)):
-        l_copy(chip_, n).wait_send()
-        l_pass(chip_, n).wait_send()
-    l_pass(chip, 3).wait_send()
+    @pl.when(jnp.logical_not(end))
+    def _():
+        for h in range(2):
+            send_back(h).wait_send()
+
     for t in range(2):
         send_far(0, t).wait_send()
         send_far(1, t).wait_send()
@@ -304,11 +377,13 @@
             scratch_shapes=[
                 vmem((1024, 128), f32), pltpu.SMEM((5, 2, 2, 5), f32),
                 vmem((4, 4, 256, 256), f32), vmem((5, 128, 1024), f32), vmem((5, 128, 1024), f32),
+                vmem((2, 5, 128, 256), f32),
                 vmem((2, 256, 1280), f32), vmem((8, 5, 128, 256), f32), vmem((8, 2, 128, 256), f32),
                 vmem((2, 128, 256), f32), vmem((2, 128, 256), f32), vmem((2, 2, 128, 256), f32),
                 vmem((2, 2, 128, 256), f32), vmem((2, 128, 256), f32),
                 sem((4, 4)), sem((4, 4)), sem((4, 4)), sem((4, 4, 2)), sem((3,)), sem((4,)), sem((8,)), sem((4,)),
                 sem((7, 2)), sem((3, 2)), sem((2, 2, 2)),
+                vmem((2, 128, 256), f32), sem((2,)), sem((2,)),
             ],
             compiler_params=pltpu.CompilerParams(collective_id=0, has_side_effects=True,
                                                  vmem_limit_bytes=53 * 1024 * 1024),

time: 69.8 us -> 65.2 us (0.934)
  Pallas kernels: 68.1 us -> 63 us
    pallas_call x1, Pallas kernels: 68.1 us -> 63 us  [local_apply(): pl.pallas_call(kernel, out_shape=jax.ShapeDtypeStruct((1024, 128), f32),...]
where the time goes in v3:
time: 65.2 us; the launch traced here: 64.5 us
  Pallas kernels  63 us (97%)
  local copies, waits for them, and re-layouts  1.5 us (2%)
    pallas_call x1, Pallas kernels, local_apply(): pl.pallas_call(kernel, out_shape=jax.ShapeDtypeStruct((1024, 128), f32),...  63 us
    unnamed x3, local copies, waits for them, and re-layouts  1.5 us

profile of v3, /device:TPU:0, one launch (start us, length us, event | category | flops | bytes accessed | tf_op | source)
XLA Modules:
  0.0 64.5 jit_solution(9889178651564658669)
XLA Ops:
  0.0 0.0 copy-start
  0.0 0.7 %copy-done = f32[5,2,2,5]{3,2,1,0:T(2,128)S(1)} copy-done((f32[5,2,2,5]{3,2,1,0:T(2,128)S(1)}, f32[5,2,2,5]{3,2,1,0:T(2,128)}, u32[]{:S(2)}) %copy-start) | copy-done | bytes 424
  0.7 63.0 %shard_map.46 = f32[1024,128]{1,0:T(8,128)S(1)} custom-call(f32[1024,128]{1,0:T(8,128)} %bitcast.15, f32[5,128,1024]{2,1,0:T(8,128)} %bitcast.14, f32[5,2,2,5]{3,2,1,0:T(2,128)S(1)} %copy-done, f32[5,256,1024]{2,1,0:T(8,128)} %bitcast.13), custom_call_target="tpu_custom_call" | custom-call | tf_op jit(solution)/shard_map/pallas_call | solution.py:371
  63.7 0.8 %copy.8 = f32[128,2,2,256]{3,2,1,0:T(2,128)} copy(f32[128,2,2,256]{3,2,1,0:T(2,128)S(1)} %bitcast.12) | data formatting | bytes 1048576
Async XLA Ops:
  0.0 0.7 %copy-start = (f32[5,2,2,5]{3,2,1,0:T(2,128)S(1)}, f32[5,2,2,5]{3,2,1,0:T(2,128)}, u32[]{:S(2)}) copy-start(f32[5,2,2,5]{3,2,1,0:T(2,128)} %w_hbm.1) | copy-start | bytes 1204

commit v4 on v3

--- a/solution.py
+++ b/solution.py
@@ -124,19 +124,21 @@
 
     def tiles(body):
         def tile(n, _):
-            body(pl.ds(pl.multiple_of(n * 8, 8), 8), n * 8)
+            body(pl.ds(pl.multiple_of(n * 16, 16), 16), n * 16)
             return 0
 
-        lax.fori_loop(0, 16, tile, 0)
-
-    def sites_first(b, start):
-        parts = [(q, r, field(r, 0, q, b)) for q in range(2) for r in range(5)]
-        for t in range(2):
+        lax.fori_loop(0, 8, tile, 0)
+
+    def sites_first(t):
+        def body(b, start):
+            parts = [(q, r, field(r, 0, q, b)) for q in range(2) for r in range(5)]
             mid = [dots((wt(v, t, q, r), x) for q, r, x in parts) for v in range(5)]
             for s in range(2):
-                into = pl.ds(pl.multiple_of(s * 128 + start, 8), 8)
+                into = pl.ds(pl.multiple_of(s * 128 + start, 16), 16)
                 for u in range(5):
                     vt[t, into, u * 256:(u + 1) * 256] = dots((wt(u, s, 0, v), mid[v]) for v in range(5))
+
+        tiles(body)
 
     def sites_second(b, start):
         parts = [field(r, 1, 0, b) for r in range(5)]
@@ -144,19 +146,55 @@
             for v in range(5):
                 zp[t, v, b, :] = dots((wt(v, t, 0, r), parts[r]) for r in range(5))
 
-    def sites_last(t):
-        def body(b, start):
-            parts = [field(r, 1, 1, b) for r in range(5)]
-            mid = [zp[t, v, b, :] + dots((wt(v, t, 1, r), parts[r]) for r in range(5)) for v in range(5)]
+    def sites_last(t, half):
+        def tile(n, _):
+            b = pl.ds(pl.multiple_of(n * 32, 32), 32)
+
+            def lanes(first):
+                return pl.ds(pl.multiple_of(first + half * 128, 128), 128)
+
+            parts = [acc[r, b, lanes(768)] for r in range(5)]
+            mid = [zp[t, v, b, lanes(0)] + dots((wt(v, t, 1, r), parts[r]) for r in range(5)) for v in range(5)]
             for s in range(2):
-                into = pl.ds(pl.multiple_of(s * 128 + start, 8), 8)
+                into = pl.ds(pl.multiple_of(s * 128 + n * 32, 32), 32)
                 for u in range(5):
-                    vt[t, into, u * 256:(u + 1) * 256] += dots((wt(u, s, 1, v), mid[v]) for v in range(5))
-
-        tiles(body)
+                    vt[t, into, lanes(u * 256)] += dots((wt(u, s, 1, v), mid[v]) for v in range(5))
+            return 0
+
+        lax.fori_loop(0, 4, tile, 0)
 
     low = j < 2
     jm = jnp.where(low, j, 3 - j)
+
+    def pass_rest():
+        for n, chip_ in ((2, dc), (1, yc)):
+            l_pass(chip_, n).wait_recv()
+            l_pass(chip_, n).start()
+
+    def wait_partner(z, q):
+        held = xg.at[z, q, other_rows, :]
+        remote(held, held, x_pt.at[z, q], x_in.at[z, q, 1 - core], partner).wait_recv()
+
+    def right_part(z):
+        return rv[:, :, pl.ds(pl.multiple_of(z * 256, 256), 256)].reshape(640, 256)
+
+    def multiply(m, _):
+        t, q = lax.div(m, 4), lax.rem(m, 4)
+        zm = jnp.where(t == 0, jm, jnp.where(t == 1, 1 - jm, t))
+        z = jnp.where(low, zm, 3 - zm)
+        wait_partner(z, q)
+        part = dot_nt(right_part(z), xg[z, q]).reshape(5, 128, 256)
+        dst = acc.at[:, :, pl.ds(pl.multiple_of(q * 256, 256), 256)]
+
+        @pl.when(t == 0)
+        def _():
+            dst[...] = part
+
+        @pl.when(t > 0)
+        def _():
+            dst[...] += part
+
+        return 0
 
     def step(n, _):
         t, q = lax.div(n, 4), lax.rem(n, 4)
@@ -185,45 +223,48 @@
 
         @pl.when(n == 12)
         def _():
-            for m, chip_ in enumerate((xc, yc)):
-                l_pass(chip_, m).wait_recv()
-                l_pass(chip_, m).start()
-
-        @pl.when(n == 15)
-        def _():
-            l_pass(dc, 2).wait_recv()
-            l_pass(dc, 2).start()
-
-        @pl.when(n > 0)
-        def _():
-            tt, qq = lax.div(n - 1, 4), lax.rem(n - 1, 4)
-            zm = jnp.where(tt == 0, jm, jnp.where(tt == 1, 1 - jm, tt))
-            z = jnp.where(low, zm, 3 - zm)
-            remote(xg.at[z, qq, other_rows, :], xg.at[z, qq, other_rows, :], x_pt.at[z, qq],
-                   x_in.at[z, qq, 1 - core], partner).wait_recv()
-            lhs = rv[:, :, pl.ds(pl.multiple_of(z * 256, 256), 256)].reshape(640, 256)
-            part = dot_nt(lhs, xg[z, qq]).reshape(5, 128, 256)
-            dst = acc.at[:, :, pl.ds(pl.multiple_of(qq * 256, 256), 256)]
-
-            @pl.when(tt == 0)
-            def _():
-                dst[...] = part
-
-            @pl.when(tt > 0)
-            def _():
-                dst[...] += part
+            l_pass(xc, 0).wait_recv()
+            l_pass(xc, 0).start()
+
+        @pl.when(n == jnp.where(end, 14, 15))
+        def _():
+            pass_rest()
 
         @pl.when(n == 14)
         def _():
-            tiles(sites_first)
-
-        @pl.when(n == 15)
+            sites_first(1)
+
+        lo = jnp.where(n < 14, jnp.maximum(n - 1, 0), n)
+        hi = jnp.where(n < 13, n, jnp.where(n < 15, n + 1, n))
+        lax.fori_loop(lo, hi, multiply, 0)
+
+        @pl.when(n == 13)
+        def _():
+            sites_first(0)
+
+        @pl.when(n == 14)
         def _():
             tiles(sites_second)
 
         return 0
 
-    lax.fori_loop(0, 17, step, 0)
+    lax.fori_loop(0, 16, step, 0)
+
+    def finish(n, _):
+        half = jnp.where(n == 0, core, 1 - core)
+        z = jnp.where(low, 3, 0)
+        at_half = pl.ds(pl.multiple_of(half * 128, 128), 128)
+
+        @pl.when(n == 1)
+        def _():
+            wait_partner(z, 3)
+
+        dst = acc.at[:, :, pl.ds(pl.multiple_of(768 + half * 128, 128), 128)]
+        dst[...] += dot_nt(right_part(z), xg[z, 3, at_half, :]).reshape(5, 128, 128)
+        sites_last(0, half)
+        return 0
+
+    lax.fori_loop(0, 2, finish, 0)
 
     def left(first, second, t):
         lhs = jnp.concatenate(
@@ -255,18 +296,24 @@
         land = ry if h else rx
         return remote(rq.at[h], land.at[core, 0], q_out.at[h], r_sem.at[h, core, 0], (pair, 2 * chip + h))
 
-    wait_left(dc)
-    wait_left(xc)
-    wait_left(yc)
-    wait_left(chip)
-
     def stage(n, _):
-        role = jnp.where(n < 4, lax.rem(n, 2), jnp.where((n == 4) | (n == 7), 3, 2))
-        t = jnp.where(n < 4, lax.div(n, 2), lax.div(n - 4, 2))
-
-        @pl.when((n == 0) | (n == 2))
-        def _():
-            sites_last(t)
+        role = jnp.where(n < 4, lax.div(n, 2), jnp.where((n == 4) | (n == 7), 3, 2))
+        t = jnp.where(n < 4, lax.rem(n, 2), lax.div(n - 4, 2))
+
+        @pl.when(n == 1)
+        def _():
+            sites_last(1, 0)
+            sites_last(1, 1)
+
+        @pl.when(n == 0)
+        def _():
+            wait_left(dc)
+            wait_left(chip)
+
+        @pl.when(n == 1)
+        def _():
+            wait_left(xc)
+            wait_left(yc)
 
         def pick(far, near, via, own):
             return jnp.where(role == 0, far, jnp.where(role == 1, near, jnp.where(role == 2, via, own)))
@@ -280,7 +327,7 @@
             pb[2 * role, t] = res[:128]
             pb[2 * role + 1, t] = res[128:]
 
-        @pl.when((n == 6) & jnp.logical_not(end))
+        @pl.when((n == 7) & jnp.logical_not(end))
         def _():
             for h in range(2):
                 send_via(h).wait_recv()

time: 65.2 us -> 62.8 us (0.963)
  Pallas kernels: 63 us -> 61.1 us
    pallas_call x1, Pallas kernels: 63 us -> 61.1 us  [local_apply(): pl.pallas_call(kernel, out_shape=jax.ShapeDtypeStruct((1024, 128), f32),...]
where the time goes in v4:
time: 62.8 us; the launch traced here: 62.6 us
  Pallas kernels  61.1 us (97%)
  local copies, waits for them, and re-layouts  1.5 us (2%)
    pallas_call x1, Pallas kernels, local_apply(): pl.pallas_call(kernel, out_shape=jax.ShapeDtypeStruct((1024, 128), f32),...  61.1 us
    unnamed x3, local copies, waits for them, and re-layouts  1.5 us

profile of v4, /device:TPU:0, one launch (start us, length us, event | category | flops | bytes accessed | tf_op | source)
XLA Modules:
  0.0 62.6 jit_solution(18286328451707058484)
XLA Ops:
  0.0 0.0 copy-start
  0.0 0.7 %copy-done = f32[5,2,2,5]{3,2,1,0:T(2,128)S(1)} copy-done((f32[5,2,2,5]{3,2,1,0:T(2,128)S(1)}, f32[5,2,2,5]{3,2,1,0:T(2,128)}, u32[]{:S(2)}) %copy-start) | copy-done | bytes 424
  0.7 61.1 %shard_map.46 = f32[1024,128]{1,0:T(8,128)S(1)} custom-call(f32[1024,128]{1,0:T(8,128)} %bitcast.15, f32[5,128,1024]{2,1,0:T(8,128)} %bitcast.14, f32[5,2,2,5]{3,2,1,0:T(2,128)S(1)} %copy-done, f32[5,256,1024]{2,1,0:T(8,128)} %bitcast.13), custom_call_target="tpu_custom_call" | custom-call | tf_op jit(solution)/shard_map/pallas_call | solution.py:418
  61.8 0.8 %copy.8 = f32[128,2,2,256]{3,2,1,0:T(2,128)} copy(f32[128,2,2,256]{3,2,1,0:T(2,128)S(1)} %bitcast.12) | data formatting | bytes 1048576
Async XLA Ops:
  0.0 0.7 %copy-start = (f32[5,2,2,5]{3,2,1,0:T(2,128)S(1)}, f32[5,2,2,5]{3,2,1,0:T(2,128)}, u32[]{:S(2)}) copy-start(f32[5,2,2,5]{3,2,1,0:T(2,128)} %w_hbm.1) | copy-start | bytes 1204

commit v5 on v4

--- a/solution.py
+++ b/solution.py
@@ -196,6 +196,11 @@
 
         return 0
 
+    def ready(n):
+        ends = jnp.where(n < 13, n, jnp.minimum(n + 1, 15))
+        mids = jnp.where(n < 8, n, jnp.where(n < 11, 2 * n - 7, jnp.minimum(n + 3, 15)))
+        return jnp.maximum(jnp.where(end, ends, mids), 0)
+
     def step(n, _):
         t, q = lax.div(n, 4), lax.rem(n, 4)
 
@@ -226,7 +231,7 @@
             l_pass(xc, 0).wait_recv()
             l_pass(xc, 0).start()
 
-        @pl.when(n == jnp.where(end, 14, 15))
+        @pl.when((n == 14) & end)
         def _():
             pass_rest()
 
@@ -234,9 +239,7 @@
         def _():
             sites_first(1)
 
-        lo = jnp.where(n < 14, jnp.maximum(n - 1, 0), n)
-        hi = jnp.where(n < 13, n, jnp.where(n < 15, n + 1, n))
-        lax.fori_loop(lo, hi, multiply, 0)
+        lax.fori_loop(ready(n - 1), ready(n), multiply, 0)
 
         @pl.when(n == 13)
         def _():
@@ -265,6 +268,11 @@
         return 0
 
     lax.fori_loop(0, 2, finish, 0)
+
+    @pl.when(jnp.logical_not(end))
+    def _():
+        pass_rest()
+
 
     def left(first, second, t):
         lhs = jnp.concatenate(
@@ -434,7 +442,7 @@
             ],
             compiler_params=pltpu.CompilerParams(collective_id=0, has_side_effects=True,
                                                  vmem_limit_bytes=53 * 1024 * 1024),
-        )(x, left.transpose(1, 0, 2), mpo, right.transpose(1, 0, 2))
+        )(x, left.transpose(1, 0, 2), pltpu.with_memory_space_constraint(mpo, pltpu.HBM), right.transpose(1, 0, 2))
         return y.reshape(128, 2, 2, 2, 128).transpose(0, 1, 3, 2, 4).reshape(128, 2, 2, 256)
 
     return jax.shard_map(local_apply, mesh=mesh,

time: 62.8 us -> 62 us (0.987)
  local copies, waits for them, and re-layouts: 1.5 us -> 0.8 us
    unnamed x3 -> x1, local copies, waits for them, and re-layouts: 1.5 us -> 0.8 us
where the time goes in v5:
time: 62 us; the launch traced here: 61.9 us
  Pallas kernels  61.1 us (99%)
  local copies, waits for them, and re-layouts  0.8 us (1%)
    pallas_call x1, Pallas kernels, local_apply(): pl.pallas_call(kernel, out_shape=jax.ShapeDtypeStruct((1024, 128), f32),...  61.1 us

profile of v5, /device:TPU:0, one launch (start us, length us, event | category | flops | bytes accessed | tf_op | source)
XLA Modules:
  0.0 61.9 jit_solution(10498784475970187854)
XLA Ops:
  0.0 61.1 %shard_map.46 = f32[1024,128]{1,0:T(8,128)S(1)} custom-call(f32[1024,128]{1,0:T(8,128)} %bitcast.15, f32[5,128,1024]{2,1,0:T(8,128)} %bitcast.14, f32[5,2,2,5]{3,2,1,0:T(2,128)} %w_hbm.1, f32[5,256,1024]{2,1,0:T(8,128)} %bitcast.13), custom_call_target="tpu_custom_call" | custom-call | tf_op jit(solution)/shard_map/pallas_call | solution.py:426
  61.1 0.8 %copy.8 = f32[128,2,2,256]{3,2,1,0:T(2,128)} copy(f32[128,2,2,256]{3,2,1,0:T(2,128)S(1)} %bitcast.12) | data formatting | bytes 1048576

commit v6 on v5

--- a/solution.py
+++ b/solution.py
@@ -77,7 +77,7 @@
         pl.semaphore_wait(barrier, 10)
 
     def x_copy(src, z, q, sems, device):
-        return remote(src, xg.at[z, q, rows, :], sems.at[z, q], x_in.at[z, q, core], device)
+        return remote(src, xg.at[z, q, rows, :], sems, x_in.at[z, q, core], device)
 
     def x_held(z, q):
         return xg.at[z, q, rows, :]
@@ -94,11 +94,11 @@
         x_copy(x_held(j, q), j, q, x_pt, partner).start()
 
     def l_copy(chip_, n):
-        return remote(l_ref.at[:, :, cols(chip_)], lg.at[i], l_out.at[n], l_in.at[i], at(chip_, core))
+        return remote(l_ref.at[:, :, cols(chip_)], lg.at[i], l_out, l_in.at[i], at(chip_, core))
 
     def l_pass(chip_, n):
         slot = 2 * chip_ + core
-        return remote(lg.at[slot], lg.at[slot], l_pt.at[n], l_in.at[slot], partner)
+        return remote(lg.at[slot], lg.at[slot], l_pt, l_in.at[slot], partner)
 
     for n, chip_ in enumerate((xc, yc, dc)):
         l_copy(chip_, n).start()
@@ -173,7 +173,7 @@
 
     def wait_partner(z, q):
         held = xg.at[z, q, other_rows, :]
-        remote(held, held, x_pt.at[z, q], x_in.at[z, q, 1 - core], partner).wait_recv()
+        remote(held, held, x_pt, x_in.at[z, q, 1 - core], partner).wait_recv()
 
     def right_part(z):
         return rv[:, :, pl.ds(pl.multiple_of(z * 256, 256), 256)].reshape(640, 256)
@@ -281,28 +281,28 @@
 
     def wait_left(chip_):
         slot = 2 * chip_ + 1 - core
-        remote(lg.at[slot], lg.at[slot], l_pt.at[0], l_in.at[slot], partner).wait_recv()
+        remote(lg.at[slot], lg.at[slot], l_pt, l_in.at[slot], partner).wait_recv()
 
     def send_far(h, t):
         if h == 0:
-            return remote(pb.at[0, t], ra.at[t], s_sem.at[0, t], p_sem.at[0, t], at(xc, core))
-        return remote(pb.at[1, t], rb.at[t], s_sem.at[1, t], p_sem.at[1, t], at(yc, core))
+            return remote(pb.at[0, t], ra.at[t], s_sem, p_sem.at[0, t], at(xc, core))
+        return remote(pb.at[1, t], rb.at[t], s_sem, p_sem.at[1, t], at(yc, core))
 
     def send_x(n, h, t):
-        return remote(pb.at[n, t], rx.at[core, t], s_sem.at[n, t], r_sem.at[0, core, t], at(xc, h))
+        return remote(pb.at[n, t], rx.at[core, t], s_sem, r_sem.at[0, core, t], at(xc, h))
 
     def send_y(n, h, t):
-        return remote(pb.at[n, t], ry.at[core, t], s_sem.at[n, t], r_sem.at[1, core, t], at(yc, h))
+        return remote(pb.at[n, t], ry.at[core, t], s_sem, r_sem.at[1, core, t], at(yc, h))
 
     def send_pt(t):
-        return remote(pb.at[6, t], rp.at[t], s_sem.at[6, t], p_sem.at[2, t], partner)
+        return remote(pb.at[6, t], rp.at[t], s_sem, p_sem.at[2, t], partner)
 
     def send_via(h):
-        return remote(pb.at[2 + h, 0], rq.at[h], s_sem.at[2 + h, 0], q_in.at[h], (pair, 2 * (yc if h else xc) + core))
+        return remote(pb.at[2 + h, 0], rq.at[h], s_sem, q_in.at[h], (pair, 2 * (yc if h else xc) + core))
 
     def send_back(h):
         land = ry if h else rx
-        return remote(rq.at[h], land.at[core, 0], q_out.at[h], r_sem.at[h, core, 0], (pair, 2 * chip + h))
+        return remote(rq.at[h], land.at[core, 0], q_out, r_sem.at[h, core, 0], (pair, 2 * chip + h))
 
     def stage(n, _):
         role = jnp.where(n < 4, lax.div(n, 2), jnp.where((n == 4) | (n == 7), 3, 2))
@@ -373,30 +373,26 @@
 
     lax.fori_loop(0, 8, stage, 0)
 
-    def drain(n, _):
-        z, q = lax.div(n, 4), lax.rem(n, 4)
-
-        @pl.when((z <= j) & (j < 3))
-        def _():
-            x_copy(x_held(z, q), z, q, x_up, (j + 1, i)).wait_send()
-
-        @pl.when((z >= j) & (j > 0))
-        def _():
-            x_copy(x_held(z, q), z, q, x_dn, (j - 1, i)).wait_send()
-
-        x_copy(x_held(z, q), z, q, x_pt, partner).wait_send()
-        return 0
-
-    lax.fori_loop(0, 16, drain, 0)
-    for n, chip_ in enumerate((xc, yc, dc)):
-        l_copy(chip_, n).wait_send()
-        l_pass(chip_, n).wait_send()
-    l_pass(chip, 3).wait_send()
+    def sent(what, sem):
+        remote(what, what, sem, l_in.at[0], partner).wait_send()
+
+    for blocks in range(1, 4):
+        @pl.when(j == blocks - 1)
+        def _():
+            sent(xg.at[pl.ds(0, blocks), :, rows, :], x_up)
+
+        @pl.when(j == 4 - blocks)
+        def _():
+            sent(xg.at[pl.ds(0, blocks), :, rows, :], x_dn)
+
+    sent(xg.at[:, :, rows, :], x_pt)
+    sent(lg.at[pl.ds(0, 3)], l_out)
+    sent(lg.at[pl.ds(0, 4)], l_pt)
     for t in range(2):
         send_pt(t).wait_recv()
         for half in range(2):
-            remote(rx.at[half, t], rx.at[half, t], s_sem.at[0, t], r_sem.at[0, half, t], partner).wait_recv()
-            remote(ry.at[half, t], ry.at[half, t], s_sem.at[0, t], r_sem.at[1, half, t], partner).wait_recv()
+            remote(rx.at[half, t], rx.at[half, t], s_sem, r_sem.at[0, half, t], partner).wait_recv()
+            remote(ry.at[half, t], ry.at[half, t], s_sem, r_sem.at[1, half, t], partner).wait_recv()
         for s in range(2):
             lanes = slice(s * 128, (s + 1) * 128)
             y_ref[pl.ds(s * 4 + core * 2 + t, 128, stride=8), :] = (
@@ -406,17 +402,9 @@
 
     @pl.when(jnp.logical_not(end))
     def _():
-        for h in range(2):
-            send_back(h).wait_send()
-
-    for t in range(2):
-        send_far(0, t).wait_send()
-        send_far(1, t).wait_send()
-        send_x(2, 0, t).wait_send()
-        send_y(3, 1, t).wait_send()
-        send_y(4, 0, t).wait_send()
-        send_x(5, 1, t).wait_send()
-        send_pt(t).wait_send()
+        sent(rq, q_out)
+
+    sent(pb.at[pl.ds(0, 7)], s_sem)
 
 
 def solution(mesh):
@@ -436,9 +424,8 @@
                 vmem((2, 256, 1280), f32), vmem((8, 5, 128, 256), f32), vmem((8, 2, 128, 256), f32),
                 vmem((2, 128, 256), f32), vmem((2, 128, 256), f32), vmem((2, 2, 128, 256), f32),
                 vmem((2, 2, 128, 256), f32), vmem((2, 128, 256), f32),
-                sem((4, 4)), sem((4, 4)), sem((4, 4)), sem((4, 4, 2)), sem((3,)), sem((4,)), sem((8,)), sem((4,)),
-                sem((7, 2)), sem((3, 2)), sem((2, 2, 2)),
-                vmem((2, 128, 256), f32), sem((2,)), sem((2,)),
+                sem, sem, sem, sem((4, 4, 2)), sem, sem, sem((8,)), sem((4,)), sem, sem((3, 2)), sem((2, 2, 2)),
+                vmem((2, 128, 256), f32), sem, sem((2,)),
             ],
             compiler_params=pltpu.CompilerParams(collective_id=0, has_side_effects=True,
                                                  vmem_limit_bytes=53 * 1024 * 1024),

time: 62 us -> 61.4 us (level)
  no operation moved by 1% of the time
where the time goes in v6:
time: 61.4 us; the launch traced here: 61.3 us
  Pallas kernels  60.5 us (99%)
  local copies, waits for them, and re-layouts  0.8 us (1%)
    pallas_call x1, Pallas kernels, local_apply(): pl.pallas_call(kernel, out_shape=jax.ShapeDtypeStruct((1024, 128), f32),...  60.5 us

profile of v6, /device:TPU:0, one launch (start us, length us, event | category | flops | bytes accessed | tf_op | source)
XLA Modules:
  0.0 61.3 jit_solution(9680666810974025969)
XLA Ops:
  0.0 60.5 %shard_map.46 = f32[1024,128]{1,0:T(8,128)S(1)} custom-call(f32[1024,128]{1,0:T(8,128)} %bitcast.15, f32[5,128,1024]{2,1,0:T(8,128)} %bitcast.14, f32[5,2,2,5]{3,2,1,0:T(2,128)} %w_hbm.1, f32[5,256,1024]{2,1,0:T(8,128)} %bitcast.13), custom_call_target="tpu_custom_call" | custom-call | tf_op jit(solution)/shard_map/pallas_call | solution.py:414
  60.5 0.8 %copy.8 = f32[128,2,2,256]{3,2,1,0:T(2,128)} copy(f32[128,2,2,256]{3,2,1,0:T(2,128)S(1)} %bitcast.12) | data formatting | bytes 1048576

commit v7 on v6

--- a/solution.py
+++ b/solution.py
@@ -17,7 +17,7 @@
 
 
 def kernel(x_ref, l_ref, w_hbm, r_ref, y_ref, xv, w_ref, xg, rv, acc, zp, vt, lg, pb, ra, rb, rx, ry, rp,
-           x_up, x_dn, x_pt, x_in, l_out, l_pt, l_in, loc, s_sem, p_sem, r_sem, rq, q_out, q_in):
+           x_up, x_dn, x_pt, x_own, x_in, l_out, l_pt, l_in, loc, s_sem, p_sem, r_sem, rq, q_out, q_in):
     j, i = lax.axis_index('by'), lax.axis_index('bx')
     chip, core = lax.div(i, 2), lax.rem(i, 2)
     xb, yb = lax.rem(chip, 2), lax.div(chip, 2)
@@ -76,8 +76,20 @@
     def _():
         pl.semaphore_wait(barrier, 10)
 
-    def x_copy(src, z, q, sems, device):
-        return remote(src, xg.at[z, q, rows, :], sems, x_in.at[z, q, core], device)
+    def x_copy(src, z, q, sems, recv, device):
+        return remote(src, xg.at[z, q, rows, :], sems, recv, device)
+
+    def up(z, q):
+        return x_copy(x_held(z, q), z, q, x_up, x_in.at[z, q, core], (j + 1, i))
+
+    def down(z, q):
+        return x_copy(x_held(z, q), z, q, x_dn, x_in.at[z - 1, q, core], (j - 1, i))
+
+    def foreign(z):
+        return jnp.where(z > j, z - 1, z)
+
+    def across(z, q):
+        return x_copy(x_held(z, q), z, q, x_pt, x_in.at[foreign(z), q, core], partner)
 
     def x_held(z, q):
         return xg.at[z, q, rows, :]
@@ -85,20 +97,24 @@
     for q in range(4):
         @pl.when(j < 3)
         def _():
-            x_copy(x_held(j, q), j, q, x_up, (j + 1, i)).start()
+            up(j, q).start()
 
         @pl.when(j > 0)
         def _():
-            x_copy(x_held(j, q), j, q, x_dn, (j - 1, i)).start()
-
-        x_copy(x_held(j, q), j, q, x_pt, partner).start()
+            down(j, q).start()
+
+        x_copy(x_held(j, q), j, q, x_pt, x_own, partner).start()
 
     def l_copy(chip_, n):
-        return remote(l_ref.at[:, :, cols(chip_)], lg.at[i], l_out, l_in.at[i], at(chip_, core))
+        return remote(l_ref.at[:, :, cols(chip_)], lg.at[i], l_out, l_in.at[min(n, 1)], at(chip_, core))
 
     def l_pass(chip_, n):
         slot = 2 * chip_ + core
-        return remote(lg.at[slot], lg.at[slot], l_pt, l_in.at[slot], partner)
+        return remote(lg.at[slot], lg.at[slot], l_pt, l_in.at[2 + n // 2], partner)
+
+    def l_wait(count, n):
+        held = lg.at[pl.ds(0, count)]
+        remote(held, held, l_pt, l_in.at[n], partner).wait_recv()
 
     for n, chip_ in enumerate((xc, yc, dc)):
         l_copy(chip_, n).start()
@@ -108,7 +124,7 @@
     load_r.wait()
 
     def arrive(z, q):
-        x_copy(x_held(z, q), z, q, x_pt, partner).wait_recv()
+        x_copy(x_held(z, q), z, q, x_pt, x_in.at[foreign(z), q, core], partner).wait_recv()
 
     def wt(u, s, p, v):
         return w_ref[u, s, p, v]
@@ -167,13 +183,13 @@
     jm = jnp.where(low, j, 3 - j)
 
     def pass_rest():
-        for n, chip_ in ((2, dc), (1, yc)):
-            l_pass(chip_, n).wait_recv()
-            l_pass(chip_, n).start()
+        l_wait(2, 1)
+        l_pass(dc, 2).start()
+        l_pass(yc, 1).start()
 
     def wait_partner(z, q):
         held = xg.at[z, q, other_rows, :]
-        remote(held, held, x_pt, x_in.at[z, q, 1 - core], partner).wait_recv()
+        remote(held, held, x_pt, x_in.at[foreign(z), q, 1 - core], partner).wait_recv()
 
     def right_part(z):
         return rv[:, :, pl.ds(pl.multiple_of(z * 256, 256), 256)].reshape(640, 256)
@@ -182,7 +198,16 @@
         t, q = lax.div(m, 4), lax.rem(m, 4)
         zm = jnp.where(t == 0, jm, jnp.where(t == 1, 1 - jm, t))
         z = jnp.where(low, zm, 3 - zm)
-        wait_partner(z, q)
+
+        @pl.when(m == 0)
+        def _():
+            held = xg.at[j, :, other_rows, :]
+            remote(held, held, x_pt, x_own, partner).wait_recv()
+
+        @pl.when(t > 0)
+        def _():
+            wait_partner(z, q)
+
         part = dot_nt(right_part(z), xg[z, q]).reshape(5, 128, 256)
         dst = acc.at[:, :, pl.ds(pl.multiple_of(q * 256, 256), 256)]
 
@@ -211,9 +236,9 @@
 
             @pl.when(j < 3)
             def _():
-                x_copy(x_held(z, q), z, q, x_up, (j + 1, i)).start()
-
-            x_copy(x_held(z, q), z, q, x_pt, partner).start()
+                up(z, q).start()
+
+            across(z, q).start()
 
         @pl.when((t > 0) & (n < 16) & (j + t <= 3))
         def _():
@@ -222,13 +247,13 @@
 
             @pl.when(j > 0)
             def _():
-                x_copy(x_held(z, q), z, q, x_dn, (j - 1, i)).start()
-
-            x_copy(x_held(z, q), z, q, x_pt, partner).start()
+                down(z, q).start()
+
+            across(z, q).start()
 
         @pl.when(n == 12)
         def _():
-            l_pass(xc, 0).wait_recv()
+            l_wait(1, 0)
             l_pass(xc, 0).start()
 
         @pl.when((n == 14) & end)
@@ -279,30 +304,26 @@
             [jnp.concatenate([lg[slot, u] for u in range(5)], axis=1) for slot in (first, second)], axis=0)
         return dot_nt(lhs, vt[t])
 
-    def wait_left(chip_):
-        slot = 2 * chip_ + 1 - core
-        remote(lg.at[slot], lg.at[slot], l_pt, l_in.at[slot], partner).wait_recv()
-
     def send_far(h, t):
         if h == 0:
-            return remote(pb.at[0, t], ra.at[t], s_sem, p_sem.at[0, t], at(xc, core))
-        return remote(pb.at[1, t], rb.at[t], s_sem, p_sem.at[1, t], at(yc, core))
+            return remote(pb.at[0, t], ra.at[t], s_sem, p_sem.at[t], at(xc, core))
+        return remote(pb.at[1, t], rb.at[t], s_sem, p_sem.at[t], at(yc, core))
 
     def send_x(n, h, t):
-        return remote(pb.at[n, t], rx.at[core, t], s_sem, r_sem.at[0, core, t], at(xc, h))
+        return remote(pb.at[n, t], rx.at[core, t], s_sem, r_sem.at[t], at(xc, h))
 
     def send_y(n, h, t):
-        return remote(pb.at[n, t], ry.at[core, t], s_sem, r_sem.at[1, core, t], at(yc, h))
+        return remote(pb.at[n, t], ry.at[core, t], s_sem, r_sem.at[t], at(yc, h))
 
     def send_pt(t):
-        return remote(pb.at[6, t], rp.at[t], s_sem, p_sem.at[2, t], partner)
+        return remote(pb.at[6, t], rp.at[t], s_sem, r_sem.at[t], partner)
 
     def send_via(h):
         return remote(pb.at[2 + h, 0], rq.at[h], s_sem, q_in.at[h], (pair, 2 * (yc if h else xc) + core))
 
     def send_back(h):
         land = ry if h else rx
-        return remote(rq.at[h], land.at[core, 0], q_out, r_sem.at[h, core, 0], (pair, 2 * chip + h))
+        return remote(rq.at[h], land.at[core, 0], q_out, r_sem.at[0], (pair, 2 * chip + h))
 
     def stage(n, _):
         role = jnp.where(n < 4, lax.div(n, 2), jnp.where((n == 4) | (n == 7), 3, 2))
@@ -315,13 +336,11 @@
 
         @pl.when(n == 0)
         def _():
-            wait_left(dc)
-            wait_left(chip)
+            l_wait(2, 3)
 
         @pl.when(n == 1)
         def _():
-            wait_left(xc)
-            wait_left(yc)
+            l_wait(2, 2)
 
         def pick(far, near, via, own):
             return jnp.where(role == 0, far, jnp.where(role == 1, near, jnp.where(role == 2, via, own)))
@@ -343,8 +362,7 @@
 
         @pl.when(role == 2)
         def _():
-            send_far(0, t).wait_recv()
-            send_far(1, t).wait_recv()
+            remote(ra, ra, s_sem, p_sem.at[t], partner).wait_recv()
             pb[4, t] = res[:128] + ra[t]
             pb[5, t] = res[128:] + rb[t]
             send_y(4, 0, t).start()
@@ -389,10 +407,8 @@
     sent(lg.at[pl.ds(0, 3)], l_out)
     sent(lg.at[pl.ds(0, 4)], l_pt)
     for t in range(2):
-        send_pt(t).wait_recv()
-        for half in range(2):
-            remote(rx.at[half, t], rx.at[half, t], s_sem, r_sem.at[0, half, t], partner).wait_recv()
-            remote(ry.at[half, t], ry.at[half, t], s_sem, r_sem.at[1, half, t], partner).wait_recv()
+        five = pb.at[pl.ds(0, 5), t]
+        remote(five, five, s_sem, r_sem.at[t], partner).wait_recv()
         for s in range(2):
             lanes = slice(s * 128, (s + 1) * 128)
             y_ref[pl.ds(s * 4 + core * 2 + t, 128, stride=8), :] = (
@@ -424,7 +440,7 @@
                 vmem((2, 256, 1280), f32), vmem((8, 5, 128, 256), f32), vmem((8, 2, 128, 256), f32),
                 vmem((2, 128, 256), f32), vmem((2, 128, 256), f32), vmem((2, 2, 128, 256), f32),
                 vmem((2, 2, 128, 256), f32), vmem((2, 128, 256), f32),
-                sem, sem, sem, sem((4, 4, 2)), sem, sem, sem((8,)), sem((4,)), sem, sem((3, 2)), sem((2, 2, 2)),
+                sem, sem, sem, sem, sem((3, 4, 2)), sem, sem, sem((4,)), sem((4,)), sem, sem((2,)), sem((2,)),
                 vmem((2, 128, 256), f32), sem, sem((2,)),
             ],
             compiler_params=pltpu.CompilerParams(collective_id=0, has_side_effects=True,

time: 61.4 us -> 61.2 us (level)
  no operation moved by 1% of the time
where the time goes in v7:
time: 61.2 us; the launch traced here: 61.1 us
  Pallas kernels  60.3 us (99%)
  local copies, waits for them, and re-layouts  0.8 us (1%)
    pallas_call x1, Pallas kernels, local_apply(): pl.pallas_call(kernel, out_shape=jax.ShapeDtypeStruct((1024, 128), f32),...  60.3 us

profile of v7, /device:TPU:0, one launch (start us, length us, event | category | flops | bytes accessed | tf_op | source)
XLA Modules:
  0.0 61.1 jit_solution(3220633603727602337)
XLA Ops:
  0.0 60.3 %shard_map.46 = f32[1024,128]{1,0:T(8,128)S(1)} custom-call(f32[1024,128]{1,0:T(8,128)} %bitcast.15, f32[5,128,1024]{2,1,0:T(8,128)} %bitcast.14, f32[5,2,2,5]{3,2,1,0:T(2,128)} %w_hbm.1, f32[5,256,1024]{2,1,0:T(8,128)} %bitcast.13), custom_call_target="tpu_custom_call" | custom-call | tf_op jit(solution)/shard_map/pallas_call | solution.py:430
  60.3 0.8 %copy.8 = f32[128,2,2,256]{3,2,1,0:T(2,128)} copy(f32[128,2,2,256]{3,2,1,0:T(2,128)S(1)} %bitcast.12) | data formatting | bytes 1048576

commit v8 on v7

--- a/solution.py
+++ b/solution.py
@@ -17,7 +17,7 @@
 
 
 def kernel(x_ref, l_ref, w_hbm, r_ref, y_ref, xv, w_ref, xg, rv, acc, zp, vt, lg, pb, ra, rb, rx, ry, rp,
-           x_up, x_dn, x_pt, x_own, x_in, l_out, l_pt, l_in, loc, s_sem, p_sem, r_sem, rq, q_out, q_in):
+           x_up, x_dn, x_pt, x_own, x_in, l_out, l_pt, l_in, loc, s_sem, p_sem, r_sem, rq, q_out, q_in, here):
     j, i = lax.axis_index('by'), lax.axis_index('bx')
     chip, core = lax.div(i, 2), lax.rem(i, 2)
     xb, yb = lax.rem(chip, 2), lax.div(chip, 2)
@@ -42,25 +42,47 @@
     load_w = pltpu.make_async_copy(w_hbm, w_ref, loc.at[3])
     load_l = pltpu.make_async_copy(l_ref.at[:, :, cols(chip)], lg.at[i], loc.at[2])
     load_x.start()
+
+    end = (j == 0) | (j == 3)
+    odd = lax.rem(j, 2)
+    pair = j + 1 - 2 * odd
+    below, above = lax.div(j + 2, 3), 1 - lax.div(j, 3)
+
+    groups = [
+        (core, [partner]),
+        (xb, [at(xc, 0), at(xc, 1)]),
+        (yb, [at(yc, 0), at(yc, 1), at(dc, core)]),
+        (odd, [(pair, 2 * xc + core), (pair, 2 * yc + core), (pair, 2 * chip + 1 - core)]),
+    ]
+    barrier = pltpu.get_barrier_semaphore()
+
+    @pl.when(j < 3)
+    def _():
+        pl.semaphore_signal(barrier, inc=1, device_id=(j + 1, i), device_id_type=MESH)
+
+    for last, peers in groups:
+        @pl.when(last == 0)
+        def _():
+            for device in peers:
+                pl.semaphore_signal(barrier, inc=1, device_id=device, device_id_type=MESH)
+
     load_w.start()
     load_r.start()
     load_l.start()
-
-    barrier = pltpu.get_barrier_semaphore()
-    end = (j == 0) | (j == 3)
-    pair = j + 1 - 2 * lax.rem(j, 2)
-    near = [partner, at(xc, 0), at(xc, 1), at(yc, 0), at(yc, 1), at(dc, core),
-            (pair, 2 * xc + core), (pair, 2 * yc + core), (pair, 2 * chip + 1 - core)]
-    for device in near:
-        pl.semaphore_signal(barrier, inc=1, device_id=device, device_id_type=MESH)
+    ahead = core + 2 * xb + 3 * yb + 3 * odd + below
+    @pl.when(ahead > 0)
+    def _():
+        pl.semaphore_wait(barrier, ahead)
 
     @pl.when(j > 0)
     def _():
-        pl.semaphore_signal(barrier, inc=1, device_id=(j - 1, i), device_id_type=MESH)
-
-    @pl.when(j < 3)
-    def _():
-        pl.semaphore_signal(barrier, inc=1, device_id=(j + 1, i), device_id_type=MESH)
+        pl.semaphore_signal(here, inc=1, device_id=(j - 1, i), device_id_type=MESH)
+
+    for last, peers in groups:
+        @pl.when(last == 1)
+        def _():
+            for device in peers:
+                pl.semaphore_signal(here, inc=1, device_id=device, device_id_type=MESH)
 
     load_x.wait()
     for p in range(2):
@@ -68,14 +90,6 @@
             for q in range(2):
                 xg[j, p * 2 + q, rows, half * 128:(half + 1) * 128] = xv[pl.ds(p * 4 + half * 2 + q, 128, stride=8), :]
 
-    @pl.when((j > 0) & (j < 3))
-    def _():
-        pl.semaphore_wait(barrier, 11)
-
-    @pl.when((j == 0) | (j == 3))
-    def _():
-        pl.semaphore_wait(barrier, 10)
-
     def x_copy(src, z, q, sems, recv, device):
         return remote(src, xg.at[z, q, rows, :], sems, recv, device)
 
@@ -94,14 +108,21 @@
     def x_held(z, q):
         return xg.at[z, q, rows, :]
 
+    @pl.when(j > 0)
+    def _():
+        for q in range(4):
+            down(j, q).start()
+
+    behind = (1 - core) + 2 * (1 - xb) + 3 * (1 - yb) + 3 * (1 - odd) + above
+
+    @pl.when(behind > 0)
+    def _():
+        pl.semaphore_wait(here, behind)
+
     for q in range(4):
         @pl.when(j < 3)
         def _():
             up(j, q).start()
-
-        @pl.when(j > 0)
-        def _():
-            down(j, q).start()
 
         x_copy(x_held(j, q), j, q, x_pt, x_own, partner).start()
 
@@ -143,7 +164,7 @@
             body(pl.ds(pl.multiple_of(n * 16, 16), 16), n * 16)
             return 0
 
-        lax.fori_loop(0, 8, tile, 0)
+        lax.fori_loop(0, 8, tile, 0, unroll=2)
 
     def sites_first(t):
         def body(b, start):
@@ -177,7 +198,7 @@
                     vt[t, into, lanes(u * 256)] += dots((wt(u, s, 1, v), mid[v]) for v in range(5))
             return 0
 
-        lax.fori_loop(0, 4, tile, 0)
+        lax.fori_loop(0, 4, tile, 0, unroll=True)
 
     low = j < 2
     jm = jnp.where(low, j, 3 - j)
@@ -441,7 +462,7 @@
                 vmem((2, 128, 256), f32), vmem((2, 128, 256), f32), vmem((2, 2, 128, 256), f32),
                 vmem((2, 2, 128, 256), f32), vmem((2, 128, 256), f32),
                 sem, sem, sem, sem, sem((3, 4, 2)), sem, sem, sem((4,)), sem((4,)), sem, sem((2,)), sem((2,)),
-                vmem((2, 128, 256), f32), sem, sem((2,)),
+                vmem((2, 128, 256), f32), sem, sem((2,)), pltpu.SemaphoreType.REGULAR,
             ],
             compiler_params=pltpu.CompilerParams(collective_id=0, has_side_effects=True,
                                                  vmem_limit_bytes=53 * 1024 * 1024),

time: 61.2 us -> 61.1 us (level)
  no operation moved by 1% of the time
where the time goes in v8:
time: 61.1 us; the launch traced here: 61 us
  Pallas kernels  60.2 us (99%)
  local copies, waits for them, and re-layouts  0.8 us (1%)
    pallas_call x1, Pallas kernels, local_apply(): pl.pallas_call(kernel, out_shape=jax.ShapeDtypeStruct((1024, 128), f32),...  60.2 us

profile of v8, /device:TPU:0, one launch (start us, length us, event | category | flops | bytes accessed | tf_op | source)
XLA Modules:
  0.0 61.0 jit_solution(5709600608556747236)
XLA Ops:
  0.0 60.2 %shard_map.46 = f32[1024,128]{1,0:T(8,128)S(1)} custom-call(f32[1024,128]{1,0:T(8,128)} %bitcast.15, f32[5,128,1024]{2,1,0:T(8,128)} %bitcast.14, f32[5,2,2,5]{3,2,1,0:T(2,128)} %w_hbm.1, f32[5,256,1024]{2,1,0:T(8,128)} %bitcast.13), custom_call_target="tpu_custom_call" | custom-call | tf_op jit(solution)/shard_map/pallas_call | solution.py:451
  60.2 0.8 %copy.8 = f32[128,2,2,256]{3,2,1,0:T(2,128)} copy(f32[128,2,2,256]{3,2,1,0:T(2,128)S(1)} %bitcast.12) | data formatting | bytes 1048576

commit v9 on v8

--- a/solution.py
+++ b/solution.py
@@ -17,7 +17,7 @@
 
 
 def kernel(x_ref, l_ref, w_hbm, r_ref, y_ref, xv, w_ref, xg, rv, acc, zp, vt, lg, pb, ra, rb, rx, ry, rp,
-           x_up, x_dn, x_pt, x_own, x_in, l_out, l_pt, l_in, loc, s_sem, p_sem, r_sem, rq, q_out, q_in, here):
+           x_up, x_pt, x_own, x_in, l_pt, l_in, loc, s_sem, p_sem, r_sem, rq, q_in, here):
     j, i = lax.axis_index('by'), lax.axis_index('bx')
     chip, core = lax.div(i, 2), lax.rem(i, 2)
     xb, yb = lax.rem(chip, 2), lax.div(chip, 2)
@@ -97,7 +97,7 @@
         return x_copy(x_held(z, q), z, q, x_up, x_in.at[z, q, core], (j + 1, i))
 
     def down(z, q):
-        return x_copy(x_held(z, q), z, q, x_dn, x_in.at[z - 1, q, core], (j - 1, i))
+        return x_copy(x_held(z, q), z, q, x_up, x_in.at[z - 1, q, core], (j - 1, i))
 
     def foreign(z):
         return jnp.where(z > j, z - 1, z)
@@ -127,7 +127,7 @@
         x_copy(x_held(j, q), j, q, x_pt, x_own, partner).start()
 
     def l_copy(chip_, n):
-        return remote(l_ref.at[:, :, cols(chip_)], lg.at[i], l_out, l_in.at[min(n, 1)], at(chip_, core))
+        return remote(l_ref.at[:, :, cols(chip_)], lg.at[i], l_pt, l_in.at[min(n, 1)], at(chip_, core))
 
     def l_pass(chip_, n):
         slot = 2 * chip_ + core
@@ -344,7 +344,7 @@
 
     def send_back(h):
         land = ry if h else rx
-        return remote(rq.at[h], land.at[core, 0], q_out, r_sem.at[0], (pair, 2 * chip + h))
+        return remote(rq.at[h], land.at[core, 0], s_sem, r_sem.at[0], (pair, 2 * chip + h))
 
     def stage(n, _):
         role = jnp.where(n < 4, lax.div(n, 2), jnp.where((n == 4) | (n == 7), 3, 2))
@@ -415,18 +415,16 @@
     def sent(what, sem):
         remote(what, what, sem, l_in.at[0], partner).wait_send()
 
-    for blocks in range(1, 4):
-        @pl.when(j == blocks - 1)
-        def _():
-            sent(xg.at[pl.ds(0, blocks), :, rows, :], x_up)
-
-        @pl.when(j == 4 - blocks)
-        def _():
-            sent(xg.at[pl.ds(0, blocks), :, rows, :], x_dn)
+    @pl.when(end)
+    def _():
+        sent(xg.at[0, :, rows, :], x_up)
+
+    @pl.when(jnp.logical_not(end))
+    def _():
+        sent(lg.at[pl.ds(0, 4)], x_up)
 
     sent(xg.at[:, :, rows, :], x_pt)
-    sent(lg.at[pl.ds(0, 3)], l_out)
-    sent(lg.at[pl.ds(0, 4)], l_pt)
+    sent(lg.at[pl.ds(0, 7)], l_pt)
     for t in range(2):
         five = pb.at[pl.ds(0, 5), t]
         remote(five, five, s_sem, r_sem.at[t], partner).wait_recv()
@@ -439,9 +437,11 @@
 
     @pl.when(jnp.logical_not(end))
     def _():
-        sent(rq, q_out)
-
-    sent(pb.at[pl.ds(0, 7)], s_sem)
+        sent(pb, s_sem)
+
+    @pl.when(end)
+    def _():
+        sent(pb.at[pl.ds(0, 7)], s_sem)
 
 
 def solution(mesh):
@@ -461,8 +461,8 @@
                 vmem((2, 256, 1280), f32), vmem((8, 5, 128, 256), f32), vmem((8, 2, 128, 256), f32),
                 vmem((2, 128, 256), f32), vmem((2, 128, 256), f32), vmem((2, 2, 128, 256), f32),
                 vmem((2, 2, 128, 256), f32), vmem((2, 128, 256), f32),
-                sem, sem, sem, sem, sem((3, 4, 2)), sem, sem, sem((4,)), sem((4,)), sem, sem((2,)), sem((2,)),
-                vmem((2, 128, 256), f32), sem, sem((2,)), pltpu.SemaphoreType.REGULAR,
+                sem, sem, sem, sem((3, 4, 2)), sem, sem((4,)), sem((4,)), sem, sem((2,)), sem((2,)),
+                vmem((2, 128, 256), f32), sem((2,)), pltpu.SemaphoreType.REGULAR,
             ],
             compiler_params=pltpu.CompilerParams(collective_id=0, has_side_effects=True,
                                                  vmem_limit_bytes=53 * 1024 * 1024),

time: 61.1 us -> 61.1 us (level)
  no operation moved by 1% of the time
where the time goes in v9:
time: 61.1 us; the launch traced here: 61 us
  Pallas kernels  60.2 us (99%)
  local copies, waits for them, and re-layouts  0.8 us (1%)
    pallas_call x1, Pallas kernels, local_apply(): pl.pallas_call(kernel, out_shape=jax.ShapeDtypeStruct((1024, 128), f32),...  60.2 us

profile of v9, /device:TPU:0, one launch (start us, length us, event | category | flops | bytes accessed | tf_op | source)
XLA Modules:
  0.0 61.0 jit_solution(16760977858877569306)
XLA Ops:
  0.0 60.2 %shard_map.46 = f32[1024,128]{1,0:T(8,128)S(1)} custom-call(f32[1024,128]{1,0:T(8,128)} %bitcast.15, f32[5,128,1024]{2,1,0:T(8,128)} %bitcast.14, f32[5,2,2,5]{3,2,1,0:T(2,128)} %w_hbm.1, f32[5,256,1024]{2,1,0:T(8,128)} %bitcast.13), custom_call_target="tpu_custom_call" | custom-call | tf_op jit(solution)/shard_map/pallas_call | solution.py:451
  60.2 0.8 %copy.8 = f32[128,2,2,256]{3,2,1,0:T(2,128)} copy(f32[128,2,2,256]{3,2,1,0:T(2,128)S(1)} %bitcast.12) | data formatting | bytes 1048576

commit v10 on v9

--- a/solution.py
+++ b/solution.py
@@ -39,8 +39,8 @@
 
     load_r = pltpu.make_async_copy(r_ref.at[:, rows, :], rv, loc.at[0])
     load_x = pltpu.make_async_copy(x_ref, xv, loc.at[1])
-    load_w = pltpu.make_async_copy(w_hbm, w_ref, loc.at[3])
-    load_l = pltpu.make_async_copy(l_ref.at[:, :, cols(chip)], lg.at[i], loc.at[2])
+    load_w = pltpu.make_async_copy(w_hbm, w_ref, loc.at[2])
+    load_l = pltpu.make_async_copy(l_ref.at[:, :, cols(chip)], lg.at[i], loc.at[0])
     load_x.start()
 
     end = (j == 0) | (j == 3)
@@ -139,10 +139,10 @@
 
     for n, chip_ in enumerate((xc, yc, dc)):
         l_copy(chip_, n).start()
-    load_l.wait()
+    both = lg.at[pl.ds(0, 5)]
+    pltpu.make_async_copy(both, both, loc.at[0]).wait()
     l_pass(chip, 3).start()
     load_w.wait()
-    load_r.wait()
 
     def arrive(z, q):
         x_copy(x_held(z, q), z, q, x_pt, x_in.at[foreign(z), q, core], partner).wait_recv()
@@ -461,7 +461,7 @@
                 vmem((2, 256, 1280), f32), vmem((8, 5, 128, 256), f32), vmem((8, 2, 128, 256), f32),
                 vmem((2, 128, 256), f32), vmem((2, 128, 256), f32), vmem((2, 2, 128, 256), f32),
                 vmem((2, 2, 128, 256), f32), vmem((2, 128, 256), f32),
-                sem, sem, sem, sem((3, 4, 2)), sem, sem((4,)), sem((4,)), sem, sem((2,)), sem((2,)),
+                sem, sem, sem, sem((3, 4, 2)), sem, sem((4,)), sem((3,)), sem, sem((2,)), sem((2,)),
                 vmem((2, 128, 256), f32), sem((2,)), pltpu.SemaphoreType.REGULAR,
             ],
             compiler_params=pltpu.CompilerParams(collective_id=0, has_side_effects=True,

time: 61.1 us -> 61.1 us (level)
  no operation moved by 1% of the time
where the time goes in v10:
time: 61.1 us; the launch traced here: 61 us
  Pallas kernels  60.1 us (98%)
  local copies, waits for them, and re-layouts  0.8 us (1%)
    pallas_call x1, Pallas kernels, local_apply(): pl.pallas_call(kernel, out_shape=jax.ShapeDtypeStruct((1024, 128), f32),...  60.1 us

profile of v10, /device:TPU:0, one launch (start us, length us, event | category | flops | bytes accessed | tf_op | source)
XLA Modules:
  0.0 61.0 jit_solution(10567646886628347850)
XLA Ops:
  0.0 60.1 %shard_map.46 = f32[1024,128]{1,0:T(8,128)S(1)} custom-call(f32[1024,128]{1,0:T(8,128)} %bitcast.15, f32[5,128,1024]{2,1,0:T(8,128)} %bitcast.14, f32[5,2,2,5]{3,2,1,0:T(2,128)} %w_hbm.1, f32[5,256,1024]{2,1,0:T(8,128)} %bitcast.13), custom_call_target="tpu_custom_call" | custom-call | tf_op jit(solution)/shard_map/pallas_call | solution.py:451
  60.2 0.8 %copy.8 = f32[128,2,2,256]{3,2,1,0:T(2,128)} copy(f32[128,2,2,256]{3,2,1,0:T(2,128)S(1)} %bitcast.12) | data formatting | bytes 1048576
